TPU v7x, 256 devices: a whole 4x4x8 slice. The times are simulated.
256 devices in a mesh: blk: 256 (over y, z, x, core).
Axes of the slice: x: 4, y: 4, z: 8, core: 2. Of those that a mesh axis runs over, the one named last changes fastest.
Arguments:
- image_features: bfloat16 [65536, 1536], P('blk'), may hold values from -0.5 to 0.5
- head_weight: bfloat16 [1536, 1152], P('blk'), may hold values from -0.15625 to 0.15625
- text_embeds: bfloat16 [65536, 1152], P('blk'), may hold values from -0.29882812 to 0.29882812
- natural_exponent_factor: float32 [1], replicated, may hold values from 1.6 to 2.6
- logit_bias: float32 [1], replicated, may hold values from -4 to -1
Outputs:
- grad_features: bfloat16 [65536, 1536], P('blk')
- grad_text: bfloat16 [65536, 1152], P('blk')
- grad_weight: float32 [1536, 1152], P('blk')
All inputs are finite; a program needn't handle non-finite values.
Results may differ from a plain program's by a relative error of at most 0.0085.
Values may be sent and summed in bfloat16 or wider, within the bound.
A program may use at most 64 MiB of HBM per device.

v0:
```python
import jax
import jax.numpy as jnp
from jax import lax
from jax.sharding import Mesh
from jax.sharding import PartitionSpec as P

S = 4
BLK = ("blk_0", "blk_1", "blk_2", "blk_3")


epsilon = 1e-06


def passed_along(block, axis, distance):
    devices = range(lax.axis_size(axis))
    route = [((i - distance) % len(devices), i) for i in devices]
    return lax.ppermute(block, axis, route)


def in_blocks(x, dim, peers):
    before, after = (x.shape[:dim], x.shape[dim + 1 :])
    return jnp.moveaxis(x.reshape(*before, peers, -1, *after), dim, 0)


def sent_and_summed(x, axis, dim):
    parts = in_blocks(x, dim, lax.axis_size(axis))
    arrived = lax.all_to_all(parts, axis, split_axis=0, concat_axis=0, tiled=True)
    return arrived.astype(jnp.float32).sum(axis=0)


def sum_by_axis(x, axes, dim):
    far, near = axes
    own = sent_and_summed(in_blocks(x, dim, lax.axis_size(far)), near, dim + 1)
    return jnp.sum(
        lax.all_to_all(own.astype(jnp.bfloat16), far, 0, 0, tiled=True).astype(jnp.float32), axis=0
    )


def normalize(rows):
    squares = jnp.sum(rows * rows, axis=1, keepdims=True)
    length = jnp.sqrt(squares + epsilon)
    return (rows / length, length)


def similarity_derivative(
    picture_sample_group,
    caption_sample_group,
    similarity_multiplier,
    neighbour_distance,
    outer_dimension_size,
):
    similarity_matrix = (
        similarity_multiplier
        * lax.dot_general(
            picture_sample_group,
            caption_sample_group,
            (((1,), (1,)), ((), ())),
            preferred_element_type=jnp.float32,
        )
        + neighbour_distance
    )
    if outer_dimension_size:
        matched = lax.broadcasted_iota(
            jnp.int32, similarity_matrix.shape, 0
        ) == lax.broadcasted_iota(jnp.int32, similarity_matrix.shape, 1)
        match_polarity = jnp.where(matched, 1.0, -1.0).astype(jnp.float32)
    else:
        match_polarity = -jnp.ones(similarity_matrix.shape, jnp.float32)
    return (
        -similarity_multiplier
        * match_polarity
        * jax.nn.sigmoid(-match_polarity * similarity_matrix)
    ).astype(jnp.bfloat16)


def project_back(grad, unit_rows, length):
    return (grad - unit_rows * jnp.sum(unit_rows * grad, axis=1, keepdims=True)) / length


def on_device(image_features, head_weight, text_embeds, natural_exponent_factor, logit_bias):
    full_weight = lax.all_gather(head_weight, BLK, axis=0, tiled=True)
    embedded = jnp.dot(image_features, full_weight, preferred_element_type=jnp.float32)
    image_unit, image_length = normalize(embedded)
    picture_embedding_mapped = image_unit.astype(jnp.bfloat16)
    text_unit, text_length = normalize(text_embeds.astype(jnp.float32))
    text_low = text_unit.astype(jnp.bfloat16)
    similarity_multiplier = jnp.exp(natural_exponent_factor[0])
    neighbour_distance = logit_bias[0]
    image_grad = jnp.zeros(image_unit.shape, jnp.float32)
    current_neighbour_tile = text_low
    for partition_portion in range(S):
        mapping_matrix = similarity_derivative(
            picture_embedding_mapped,
            current_neighbour_tile,
            similarity_multiplier,
            neighbour_distance,
            partition_portion == 0,
        )
        image_grad = image_grad + jnp.dot(
            mapping_matrix, current_neighbour_tile, preferred_element_type=jnp.float32
        )
        if partition_portion + 1 < S:
            current_neighbour_tile = passed_along(current_neighbour_tile, BLK, -1)
    text_grad = jnp.zeros(text_unit.shape, jnp.float32)
    passing = picture_embedding_mapped
    for partition_portion in range(S):
        mapping_matrix = similarity_derivative(
            passing, text_low, similarity_multiplier, neighbour_distance, partition_portion == 0
        )
        text_grad = text_grad + lax.dot_general(
            mapping_matrix, passing, (((0,), (0,)), ((), ())), preferred_element_type=jnp.float32
        )
        if partition_portion + 1 < S:
            passing = passed_along(passing, BLK, 1)
    embed_grad = project_back(image_grad, image_unit, image_length).astype(jnp.bfloat16)
    grad_text = project_back(text_grad, text_unit, text_length).astype(jnp.bfloat16)
    grad_features = lax.dot_general(
        embed_grad, full_weight, (((1,), (1,)), ((), ())), preferred_element_type=jnp.float32
    ).astype(jnp.bfloat16)
    grad_weight = sum_by_axis(
        lax.dot_general(
            image_features, embed_grad, (((0,), (0,)), ((), ())), preferred_element_type=jnp.float32
        ).astype(jnp.bfloat16),
        (("blk_0", "blk_1"), ("blk_2", "blk_3")),
        0,
    )
    return (grad_features, grad_text, grad_weight)


def solution(mesh):
    finer = Mesh(mesh.devices.reshape(4, 8, 4, 2), ("blk_0", "blk_1", "blk_2", "blk_3"))
    return jax.shard_map(
        on_device,
        mesh=finer,
        in_specs=(P(BLK, None), P(BLK, None), P(BLK, None), P(), P()),
        out_specs=(P(BLK, None), P(BLK, None), P(BLK, None)),
        check_vma=False,
    )
```

profile of v0, /device:TPU:1, one launch (start us, length us, event | category | flops | bytes accessed | tf_op | source)
XLA Modules:
  0.0 278.5 jit_solution(11349202122939430246)
XLA Ops:
  7.2 0.0 copy-start
  7.2 0.0 all-gather.3.cloned.1.call-start
  7.2 0.7 all-gather.3.cloned.1.call-update
  7.9 1.3 fusion.1
  9.2 1.3 fusion.82
  10.5 3.3 %collective-permute-start = (bf16[256,1152]{1,0:T(8,128)(2,1)S(1)}, bf16[256,1152]{1,0:T(8,128)(2,1)S(1)}, u32[]{:S(2)}, u32[]{:S(2)}) collective-permute-start(bf16[256,1152]{1,0:T(8,128)(2,1)S(1)} %fusion.82), channel_id=1, source_target_pairs={{1,0},{2,1},{3,2},{4,3},{5,4},{6,5},{7,6},{8,7},{9,8},{10,9},{11,1... | collective-permute-start | bytes 1769480 | tf_op jit(solution)/shard_map/ppermute | solution.py:17
  13.8 7.0 %collective-permute-done = bf16[256,1152]{1,0:T(8,128)(2,1)S(1)} collective-permute-done((bf16[256,1152]{1,0:T(8,128)(2,1)S(1)}, bf16[256,1152]{1,0:T(8,128)(2,1)S(1)}, u32[]{:S(2)}, u32[]{:S(2)}) %collective-permute-start) | collective-permute-done | bytes 589856 | tf_op jit(solution)/shard_map/ppermute | solution.py:17
  20.7 8.7 %collective-permute-start.1 = (bf16[256,1152]{1,0:T(8,128)(2,1)S(1)}, bf16[256,1152]{1,0:T(8,128)(2,1)}, u32[]{:S(2)}, u32[]{:S(2)}) collective-permute-start(bf16[256,1152]{1,0:T(8,128)(2,1)S(1)} %collective-permute-done), channel_id=1, source_target_pairs={{1,0},{2,1},{3,2},{4,3},{5,4},{6,5},{7,6},{8,7},{9,8},{10,9},{11,1... | collective-permute-start | bytes 1769480 | tf_op jit(solution)/shard_map/ppermute | solution.py:17
  30.7 0.4 collective-permute-done.1
  31.2 13.1 %collective-permute-start.2 = (bf16[256,1152]{1,0:T(8,128)(2,1)}, bf16[256,1152]{1,0:T(8,128)(2,1)}, u32[]{:S(2)}, u32[]{:S(2)}) collective-permute-start(bf16[256,1152]{1,0:T(8,128)(2,1)} %collective-permute-done.1), channel_id=1, source_target_pairs={{1,0},{2,1},{3,2},{4,3},{5,4},{6,5},{7,6},{8,7},{9,8},{10,9},{11,1... | collective-permute-start | bytes 1769480 | tf_op jit(solution)/shard_map/ppermute | solution.py:17
  44.3 87.6 %all-gather.3.cloned.1.call-done = bf16[256,6,1152]{2,1,0:T(8,128)(2,1)} async-done(((bf16[1,6,1152]{2,1,0:T(8,128)(2,1)}), bf16[256,6,1152]{2,1,0:T(8,128)(2,1)}) %all-gather.3.cloned.1.call-update) | async-done | bytes 3538960 | tf_op jit(solution)/shard_map/all_gather | solution.py:81
  131.9 6.8 %reshape.22 = bf16[1536,1152]{1,0:T(8,128)(2,1)} reshape(bf16[256,6,1152]{2,1,0:T(8,128)(2,1)} %all-gather.3.cloned.1.call-done) | data formatting | bytes 7077888
  138.7 0.0 copy-done.2
  138.7 0.0 copy-done
  138.7 3.3 %multiply_reduce_fusion.2 = (f32[256]{0:T(256)S(1)}, f32[256,1152]{1,0:T(8,128)S(1)}) fusion(bf16[256,1536]{1,0:T(8,128)(2,1)S(1)} %copy-done, bf16[1536,1152]{1,0:T(8,128)(2,1)} %reshape.22), kind=kOutput, calls=%fused_computation.17 | convolution fusion | flops 906559232 | bytes 5506048 | tf_op jit(solution)/shard_map/dot_general | solution.py:82
  142.0 0.1 fusion.83
  142.2 0.4 fusion.45
  142.6 0.5 copy-done.4
  143.0 1.4 fusion.84
  144.5 2.6 convolution_add_fusion.5
  147.1 3.2 %convolution_add_fusion.4 = f32[256,1152]{1,0:T(8,128)} fusion(f32[256,1152]{1,0:T(8,128)S(1)} %convolution_add_fusion.5, bf16[256,1152]{1,0:T(8,128)(2,1)} %collective-permute-done.1, bf16[256,1152]{1,0:T(8,128)(2,1)S(1)} %fusion.83, f32[]{:T(128)S(6)} %mul.119, f32[]{:T(128)} %bitcast.39, f32[]{:T(128)} %bitcast), kind=kOutput, calls=%fused_computation.6 | convolution fusion | flops 302743552 | bytes 3538956 | tf_op jit(solution)/shard_map/dot_general | solution.py:99
  150.3 0.0 collective-permute-done.2
  150.3 4.1 %multiply_reduce_fusion.1 = (f32[256]{0:T(256)S(1)}, f32[256,1152]{1,0:T(8,128)}) fusion(f32[256,1152]{1,0:T(8,128)} %copy-done.4, f32[256]{0:T(256)S(1)} %add_sqrt_fusion.1, f32[256,1152]{1,0:T(8,128)} %convolution_add_fusion.4, bf16[256,1152]{1,0:T(8,128)(2,1)} %collective-permute-done.2, bf16[256,1152]{1,0:T(8,128)(2,1)S(1)} %fusion.83, f32[]{:T(128)S(6)} %mul.119, ...), kind=kOutput, calls=%fused_computation.16 | convolution fusion | flops 303628032 | bytes 4720652 | tf_op jit(solution)/shard_map/dot_general | solution.py:99
  154.4 4.3 %fusion = bf16[1536,1152]{0,1:T(8,128)(2,1)} fusion(bf16[256,1536]{1,0:T(8,128)(2,1)S(1)} %copy-done, f32[256,1152]{1,0:T(8,128)} %get-tuple-element.6, f32[256]{0:T(256)S(1)} %get-tuple-element.5, f32[256]{0:T(256)S(1)} %add_sqrt_fusion.1, f32[256,1152]{1,0:T(8,128)S(1)} %copy-done.5), kind=kOutput, calls=%fused_computation.1 | convolution fusion | flops 909213696 | bytes 6686720 | tf_op jit(solution)/shard_map/dot_general | solution.py:121
  158.7 5.8 %copy.13 = bf16[1536,1152]{1,0:T(8,128)(2,1)} copy(bf16[1536,1152]{0,1:T(8,128)(2,1)} %fusion) | data formatting | bytes 7077888 | tf_op jit(solution)/shard_map/convert_element_type | solution.py:123
  164.5 6.7 %reshape_reshape.3 = bf16[32,8,6,1152]{3,2,1,0:T(8,128)(2,1)} reshape(bf16[1536,1152]{1,0:T(8,128)(2,1)} %copy.13) | data formatting | bytes 7077888 | tf_op jit(solution)/shard_map/reshape;reshape | solution.py:22
  171.2 6.2 %copy.14 = bf16[8,32,6,1152]{3,1,2,0:T(8,128)(2,1)} copy(bf16[8,32,6,1152]{3,2,0,1:T(8,128)(2,1)} %bitcast.41) | data formatting | bytes 7077888 | tf_op jit(solution)/shard_map/transpose | solution.py:22
  177.3 4.6 %all-to-all-start = ((bf16[8,32,6,1152]{3,1,2,0:T(8,128)(2,1)}), bf16[8,32,6,1152]{3,1,2,0:T(8,128)(2,1)}, u32[]{:S(2)}, u32[]{:S(2)}) async-start(bf16[8,32,6,1152]{3,1,2,0:T(8,128)(2,1)} %copy.14), calls=%async_computation | async-start | bytes 7077888 | tf_op jit(solution)/shard_map/all_to_all | solution.py:27
  182.0 1.6 collective-permute-start.3
  183.6 1.4 fusion.85
  185.0 42.0 %collective-permute-done.3 = bf16[256,1152]{1,0:T(8,128)(2,1)S(1)} collective-permute-done((bf16[256,1152]{1,0:T(8,128)(2,1)S(1)}, bf16[256,1152]{1,0:T(8,128)(2,1)S(1)}, u32[]{:S(2)}, u32[]{:S(2)}) %collective-permute-start.3) | collective-permute-done | bytes 589856 | tf_op jit(solution)/shard_map/ppermute | solution.py:17
  227.0 2.5 collective-permute-start.4
  229.4 4.5 %convolution_convert_fusion.1 = bf16[256,1536]{1,0:T(8,128)(2,1)} fusion(bf16[1536,1152]{1,0:T(8,128)(2,1)} %reshape.22, f32[256,1152]{1,0:T(8,128)} %get-tuple-element.6, f32[256]{0:T(256)S(1)} %get-tuple-element.5, f32[256]{0:T(256)S(1)} %add_sqrt_fusion.1, f32[256,1152]{1,0:T(8,128)S(1)} %copy-done.6), kind=kOutput, calls=%fused_computation.8 | convolution fusion | flops 907837440 | bytes 6686720 | tf_op jit(solution)/shard_map/dot_general | solution.py:117
  233.9 2.3 collective-permute-done.4
  236.3 2.5 collective-permute-start.5
  238.8 2.7 convolution_add_fusion.2
  241.4 2.1 convolution_add_fusion.1
  243.5 0.0 all-to-all-done
  243.5 2.5 reduce_sum.61
  246.0 0.0 copy-start.1
  246.0 1.0 copy.15
  247.0 7.0 %all-to-all-start.1 = ((bf16[32,6,1152]{2,1,0:T(8,128)(2,1)}), bf16[32,6,1152]{2,1,0:T(8,128)(2,1)S(1)}, u32[]{:S(2)}, u32[]{:S(2)}) async-start(bf16[32,6,1152]{2,1,0:T(8,128)(2,1)} %copy.15), calls=%async_computation.1 | async-start | bytes 1179648 | tf_op jit(solution)/shard_map/all_to_all | solution.py:35
  254.0 0.0 collective-permute-done.5
  254.0 0.0 copy-done.1
  254.0 3.7 %multiply_reduce_fusion = (f32[256]{0:T(256)S(1)}, f32[256,1152]{1,0:T(8,128)}) fusion(f32[256]{0:T(256)S(1)} %add_sqrt_fusion, bf16[256,1152]{1,0:T(8,128)(2,1)S(1)} %copy-done.1, f32[256,1152]{1,0:T(8,128)} %convolution_add_fusion.1, bf16[256,1152]{1,0:T(8,128)(2,1)} %collective-permute-done.5, bf16[256,1152]{1,0:T(8,128)(2,1)S(1)} %fusion.82, ...), kind=kOutput, calls=%fused_computation.14 | convolution fusion | flops 303922944 | bytes 4130828 | tf_op jit(solution)/shard_map/dot_general | solution.py:110
  257.7 2.4 divide_convert_fusion
  260.1 10.9 %all-to-all-done.1 = bf16[32,6,1152]{2,1,0:T(8,128)(2,1)S(1)} async-done(((bf16[32,6,1152]{2,1,0:T(8,128)(2,1)}), bf16[32,6,1152]{2,1,0:T(8,128)(2,1)S(1)}, u32[]{:S(2)}, u32[]{:S(2)}) %all-to-all-start.1) | async-done | bytes 442400 | tf_op jit(solution)/shard_map/all_to_all | solution.py:35
  271.0 0.7 convert_reduce_fusion
  (10 shorter events, 0.0 us)
Async XLA Ops:
  7.2 131.5 %copy-start = (bf16[256,1536]{1,0:T(8,128)(2,1)S(1)}, bf16[256,1536]{1,0:T(8,128)(2,1)}, u32[]{:S(2)}) copy-start(bf16[256,1536]{1,0:T(8,128)(2,1)} %param.5) | copy-start | bytes 2359300
  7.2 124.7 %all-gather.3.cloned.1.call-start = ((), (), s32[]{:S(2)}) async-start(), calls=%async_computation.2 | async-start | bytes 4737024 | tf_op jit(solution)/shard_map/all_gather | solution.py:81
  10.5 10.2 %collective-permute-start = (bf16[256,1152]{1,0:T(8,128)(2,1)S(1)}, bf16[256,1152]{1,0:T(8,128)(2,1)S(1)}, u32[]{:S(2)}, u32[]{:S(2)}) collective-permute-start(bf16[256,1152]{1,0:T(8,128)(2,1)S(1)} %fusion.82), channel_id=1, source_target_pairs={{1,0},{2,1},{3,2},{4,3},{5,4},{6,5},{7,6},{8,7},{9,8},{10,9},{11,1... | collective-permute-start | bytes 1769480 | tf_op jit(solution)/shard_map/ppermute | solution.py:17
  20.7 118.0 %copy-start.2 = (bf16[256,1152]{1,0:T(8,128)(2,1)}, bf16[256,1152]{1,0:T(8,128)(2,1)S(1)}, u32[]{:S(2)}) copy-start(bf16[256,1152]{1,0:T(8,128)(2,1)S(1)} %collective-permute-done) | copy-start | bytes 1769476
  20.7 10.4 %collective-permute-start.1 = (bf16[256,1152]{1,0:T(8,128)(2,1)S(1)}, bf16[256,1152]{1,0:T(8,128)(2,1)}, u32[]{:S(2)}, u32[]{:S(2)}) collective-permute-start(bf16[256,1152]{1,0:T(8,128)(2,1)S(1)} %collective-permute-done), channel_id=1, source_target_pairs={{1,0},{2,1},{3,2},{4,3},{5,4},{6,5},{7,6},{8,7},{9,8},{10,9},{11,1... | collective-permute-start | bytes 1769480 | tf_op jit(solution)/shard_map/ppermute | solution.py:17
  31.2 119.1 %collective-permute-start.2 = (bf16[256,1152]{1,0:T(8,128)(2,1)}, bf16[256,1152]{1,0:T(8,128)(2,1)}, u32[]{:S(2)}, u32[]{:S(2)}) collective-permute-start(bf16[256,1152]{1,0:T(8,128)(2,1)} %collective-permute-done.1), channel_id=1, source_target_pairs={{1,0},{2,1},{3,2},{4,3},{5,4},{6,5},{7,6},{8,7},{9,8},{10,9},{11,1... | collective-permute-start | bytes 1769480 | tf_op jit(solution)/shard_map/ppermute | solution.py:17
  142.0 1.1 copy-start.4
  150.3 4.1 %copy-start.5 = (f32[256,1152]{1,0:T(8,128)S(1)}, f32[256,1152]{1,0:T(8,128)}, u32[]{:S(2)}) copy-start(f32[256,1152]{1,0:T(8,128)} %copy-done.4) | copy-start | bytes 3538948
  177.3 66.2 %all-to-all-start = ((bf16[8,32,6,1152]{3,1,2,0:T(8,128)(2,1)}), bf16[8,32,6,1152]{3,1,2,0:T(8,128)(2,1)}, u32[]{:S(2)}, u32[]{:S(2)}) async-start(bf16[8,32,6,1152]{3,1,2,0:T(8,128)(2,1)} %copy.14), calls=%async_computation | async-start | bytes 7077888 | tf_op jit(solution)/shard_map/all_to_all | solution.py:27
  182.0 47.5 %copy-start.6 = (f32[256,1152]{1,0:T(8,128)S(1)}, f32[256,1152]{1,0:T(8,128)}, u32[]{:S(2)}) copy-start(f32[256,1152]{1,0:T(8,128)} %copy-done.4) | copy-start | bytes 3538948
  182.0 45.0 %collective-permute-start.3 = (bf16[256,1152]{1,0:T(8,128)(2,1)S(1)}, bf16[256,1152]{1,0:T(8,128)(2,1)S(1)}, u32[]{:S(2)}, u32[]{:S(2)}) collective-permute-start(bf16[256,1152]{1,0:T(8,128)(2,1)S(1)} %fusion.83), channel_id=1, source_target_pairs={{255,0},{0,1},{1,2},{2,3},{3,4},{4,5},{5,6},{6,7},{7,8},{8,9},{9,1... | collective-permute-start | bytes 1769480 | tf_op jit(solution)/shard_map/ppermute | solution.py:17
  227.0 7.0 %copy-start.3 = (bf16[256,1152]{1,0:T(8,128)(2,1)}, bf16[256,1152]{1,0:T(8,128)(2,1)S(1)}, u32[]{:S(2)}) copy-start(bf16[256,1152]{1,0:T(8,128)(2,1)S(1)} %collective-permute-done.3) | copy-start | bytes 1769476
  227.0 9.3 %collective-permute-start.4 = (bf16[256,1152]{1,0:T(8,128)(2,1)S(1)}, bf16[256,1152]{1,0:T(8,128)(2,1)S(1)}, u32[]{:S(2)}, u32[]{:S(2)}) collective-permute-start(bf16[256,1152]{1,0:T(8,128)(2,1)S(1)} %collective-permute-done.3), channel_id=1, source_target_pairs={{255,0},{0,1},{1,2},{2,3},{3,4},{4,5},{5,6},{6,7},{7,8},{8,9},{9,1... | collective-permute-start | bytes 1769480 | tf_op jit(solution)/shard_map/ppermute | solution.py:17
  236.3 17.7 %collective-permute-start.5 = (bf16[256,1152]{1,0:T(8,128)(2,1)S(1)}, bf16[256,1152]{1,0:T(8,128)(2,1)}, u32[]{:S(2)}, u32[]{:S(2)}) collective-permute-start(bf16[256,1152]{1,0:T(8,128)(2,1)S(1)} %collective-permute-done.4), channel_id=1, source_target_pairs={{255,0},{0,1},{1,2},{2,3},{3,4},{4,5},{5,6},{6,7},{7,8},{8,9},{9,1... | collective-permute-start | bytes 1769480 | tf_op jit(solution)/shard_map/ppermute | solution.py:17
  246.0 8.0 %copy-start.1 = (bf16[256,1152]{1,0:T(8,128)(2,1)S(1)}, bf16[256,1152]{1,0:T(8,128)(2,1)}, u32[]{:S(2)}) copy-start(bf16[256,1152]{1,0:T(8,128)(2,1)} %param.7) | copy-start | bytes 1769476
  247.0 24.0 %all-to-all-start.1 = ((bf16[32,6,1152]{2,1,0:T(8,128)(2,1)}), bf16[32,6,1152]{2,1,0:T(8,128)(2,1)S(1)}, u32[]{:S(2)}, u32[]{:S(2)}) async-start(bf16[32,6,1152]{2,1,0:T(8,128)(2,1)} %copy.15), calls=%async_computation.1 | async-start | bytes 1179648 | tf_op jit(solution)/shard_map/all_to_all | solution.py:35
Sparse Core Ops, SparseCore 0:
  11.8 120.0 all-gather.2
where the time goes:
time: 281 us; the launch traced here: 279 us
  waiting for transfers between devices  151 us (54%)
  starting transfers between devices  43.3 us (15%)
  matrix products  33.6 us (12%)
  local copies, waits for them, and re-layouts  26.9 us (10%)
  between operations  15.5 us (6%)
  other arithmetic  8.36 us (3%)
    all_gather x1, waiting for transfers between devices, on_device(): full_weight = lax.all_gather(head_weight, BLK, axis=0, tiled=True)  87.6 us
    ppermute x6, waiting for transfers between devices, passed_along(): return lax.ppermute(block, axis, route)  51.7 us
    ppermute x6, starting transfers between devices, passed_along(): return lax.ppermute(block, axis, route)  31.7 us
    dot_general x4, matrix products, on_device(): jnp.dot(mapping_matrix, current_neighbour_tile, preferred_element_type=jn...  11.3 us
    all_to_all x1, waiting for transfers between devices, sum_by_axis(): lax.all_to_all(own.astype(jnp.bfloat16), far, 0, 0, tiled=True)  10.9 us
    dot_general x4, matrix products, on_device(): lax.dot_general(mapping_matrix, passing, (((0,), (0,)), ((), ())), prefer...  9.82 us
    unnamed x15, local copies, waits for them, and re-layouts  7.3 us
    all_to_all x1, starting transfers between devices, sum_by_axis(): lax.all_to_all(own.astype(jnp.bfloat16), far, 0, 0, tiled=True)  6.96 us
  transfers between devices with their start and end apart: 9, of which 6 were waited for; matrix products, arithmetic and copies ran while one was open for 15% of the time, Pallas kernels for 0%

commit v1 on v0

v1 whole, which is shorter than its diff:
```python
import jax
import jax.numpy as jnp
from jax import lax
from jax.experimental import pallas as pl
from jax.experimental.pallas import tpu as pltpu
from jax.sharding import PartitionSpec as P

MESH = pl.DeviceIdType.MESH
D, E, R, S = 1536, 1152, 256, 4
NY, NZ, NX = 4, 8, 4
N = NY * NZ * NX * 2
ROW = NX * 2
SH = D // N
BLK = SH * ROW
YROWS = BLK * NZ
W1 = 640
COLS = ((W1, E - W1), (0, W1))
EPS = 1e-06
F32, BF16 = jnp.float32, jnp.bfloat16
Z_ORDER = (4, 3, 5, 2, 6, 1, 7)
Z_ARRIVAL = (0, 1, 7, 2, 6, 3, 5, 4)
ORDER_NT = (((1,), (1,)), ((), ()))


def dot(a, b):
    return jnp.dot(a, b, preferred_element_type=F32)


def dot_nt(a, b):
    return lax.dot_general(a, b, ORDER_NT, preferred_element_type=F32)


def kernel(
    feat_hbm, w_hbm, text_hbm, nef_ref, bias_ref,
    gf_hbm, gt_hbm, gw_hbm,
    w_ref, feat, feat2, feat_t, unit, length, img, traw, tlow, tlen, pair, eg, gfeat, gtext,
    gpart, xbuf, wrow, rbuf, sbuf, xrow, xs, xr, gout,
    in_sem, out_sem, xw_s, xw_r, ag_s, ag_r, dd_s, dd_r, ex_s, ex_r, rs_s, rs_r, xg_s, xg_r,
):
    me = lax.axis_index("blk")
    core = lax.rem(me, 2)
    r = lax.rem(me, ROW)
    z = lax.rem(lax.div(me, ROW), NZ)
    y = lax.div(me, ROW * NZ)
    pending = []

    def dev(dy=0, dz=0):
        return (lax.rem(y + (dy + NY) , NY) * NZ + lax.rem(z + (dz + NZ), NZ)) * ROW + r

    def row_dev(k):
        return me - r + lax.rem(r + k, ROW)

    def near(k):
        return lax.rem(me + (k + N), N)

    def remote(src, dst, ss, rs, to):
        return pltpu.make_async_remote_copy(
            src_ref=src, dst_ref=dst, send_sem=ss, recv_sem=rs, device_id=(to,), device_id_type=MESH
        )

    def send(only, src, dst, ss, rs, to, like=None):
        sems, i = ss
        remote(src, dst, sems.at[i], rs, to).start()

        def wait():
            ref = src if like is None else like()
            remote(ref, ref, sems.at[i], sems.at[i], near(1)).wait_send()

        pending.append((only, wait))

    def arrived(dst, ss, rs):
        remote(dst, dst, ss, rs, near(1)).wait_recv()

    def wblock(ref, yy, zz, c0, cw):
        start = pl.multiple_of(lax.rem(yy, NY) * YROWS + lax.rem(zz, NZ) * BLK, 8)
        return ref.at[pl.ds(start, BLK), pl.ds(c0, cw)]

    cp_w = pltpu.make_async_copy(w_hbm, xbuf.at[r], in_sem.at[0])
    cp_t = pltpu.make_async_copy(text_hbm, traw.at[0], in_sem.at[1])
    cp_f = pltpu.make_async_copy(feat_hbm, feat, in_sem.at[2])
    cp_w.start()
    cp_t.start()
    cp_f.start()

    barrier = pltpu.get_barrier_semaphore()
    peers = [row_dev(k) for k in range(1, ROW)] + [dev(dz=k) for k in range(1, NZ)]
    peers += [dev(dy=k) for k in range(1, NY)] + [near(k) for k in (-3, -2, -1, 1, 2, 3)]
    for peer in peers:
        pl.semaphore_signal(barrier, inc=1, device_id=(peer,), device_id_type=MESH)
    pl.semaphore_wait(barrier, len(peers))

    cp_w.wait()
    for k in (4, 3, 5, 2, 6, 1, 7):
        send(None, xbuf.at[r], xbuf.at[r], (xw_s, k), xw_r.at[k], row_dev(k), lambda: xbuf.at[0])

    cp_t.wait()

    @pl.when(core == 0)
    def _():
        send(0, traw.at[0], traw.at[1], (ex_s, 0), ex_r.at[1], near(-1), lambda: traw.at[0])
        send(0, traw.at[0], traw.at[3], (ex_s, 1), ex_r.at[3], near(-3), lambda: traw.at[0])

    @pl.when(core == 1)
    def _():
        send(1, traw.at[0], traw.at[1], (ex_s, 0), ex_r.at[1], near(-1), lambda: traw.at[0])
        send(1, traw.at[0], traw.at[2], (ex_s, 1), ex_r.at[2], near(-2), lambda: traw.at[0])

    cp_f.wait()
    send(None, feat, feat2, (ex_s, 4), ex_r.at[0], me + 1 - 2 * core)

    for k in range(1, ROW):
        arrived(xbuf.at[lax.rem(r + (ROW - k), ROW)], xw_s.at[k], xw_r.at[k])
    for k in range(ROW):
        wrow[pl.ds(SH * k, SH), :] = xbuf[k].astype(F32)
    own = pl.multiple_of(y * YROWS + z * BLK, 8)
    w_ref[pl.ds(own, BLK), :] = wrow[...].astype(BF16)

    def gather(c):
        c0, cw = COLS[c]
        sibling = me + (1 - 2 * c)
        count = [0]
        like = lambda: w_ref.at[pl.ds(0, BLK), pl.ds(c0, cw)]

        def put(j, k, dy, dz):
            part = wblock(w_ref, y + (NY - j), z + (NZ - k), c0, cw)
            idx = ((j + dy) % NY) * NZ + (k + dz) % NZ
            send(c, part, part, (ag_s, count[0]), ag_r.at[idx], dev(dy, dz), like)
            count[0] += 1

        def share(j, k):
            part = wblock(w_ref, y + (NY - j), z + (NZ - k), c0, cw)
            send(c, part, part, (dd_s, j * NZ + k), dd_r.at[j * NZ + k], sibling, like)

        def got(j, k):
            part = wblock(w_ref, y + (NY - j), z + (NZ - k), c0, cw)
            arrived(part, ag_s.at[0], ag_r.at[j * NZ + k])
            return part

        if c == 1:
            for k in Z_ORDER:
                put(0, 0, 0, k)

            def stage1(i):
                k = Z_ARRIVAL[i]
                if k:
                    got(0, k)
                put(0, k, 1, 0)
                put(0, k, -1, 0)
                if k:
                    share(0, k)

            def stage2(i):
                k = Z_ARRIVAL[i]
                got(1, k)
                if i % 2 == 0:
                    put(1, k, 1, 0)
                share(1, k)
                got(3, k)
                if i % 2 == 1:
                    put(3, k, -1, 0)
                share(3, k)

            def stage3(i):
                k = Z_ARRIVAL[i]
                got(2, k)
                share(2, k)

            for i in range(NZ + 4):
                if i < NZ:
                    stage1(i)
                if 2 <= i < NZ + 2:
                    stage2(i - 2)
                if 4 <= i:
                    stage3(i - 4)
        else:
            for j in (2, 1, 3):
                put(0, 0, j, 0)
            for j in (0, 1, 3, 2):
                if j:
                    got(j, 0)
                put(j, 0, 0, 1)
                put(j, 0, 0, -1)
                if j:
                    share(j, 0)
            for h in (1, 2, 3):
                for j in (0, 1, 3, 2):
                    got(j, h)
                    if h < 3 or j in (0, 3):
                        put(j, h, 0, 1)
                    share(j, h)
                    got(j, NZ - h)
                    if h < 3 or j in (1, 2):
                        put(j, NZ - h, 0, -1)
                    share(j, NZ - h)
            for j in (0, 1, 3, 2):
                got(j, 4)
                share(j, 4)
        o0, ow = COLS[1 - c]
        if c == 1:
            arrived(traw.at[1], ex_s.at[0], ex_r.at[1])
            send(1, traw.at[1], traw.at[2], (ex_s, 2), ex_r.at[2], near(-1), lambda: traw.at[0])
            arrived(traw.at[2], ex_s.at[0], ex_r.at[2])
            send(1, traw.at[2], traw.at[3], (ex_s, 3), ex_r.at[3], near(-1), lambda: traw.at[0])
        for j in range(NY):
            for k in range(NZ):
                if j or k:
                    part = wblock(w_ref, y + (NY - j), z + (NZ - k), o0, ow)
                    arrived(part, dd_s.at[0], dd_r.at[j * NZ + k])

    def text_norm(s):
        @pl.loop(0, R // 32)
        def _(i):
            rows = pl.ds(pl.multiple_of(i * 32, 32), 32)
            t = traw[s, rows, :].astype(F32)
            inv = 1.0 / jnp.sqrt(jnp.sum(t * t, axis=1, keepdims=True) + EPS)
            tlow[pl.ds(pl.multiple_of(s * R + i * 32, 32), 32), :] = (t * inv).astype(BF16)
            if s == 0:
                tlen[rows, :] = inv

    def transpose(src, col):
        @pl.loop(0, D // 256)
        def _(i):
            cols = pl.ds(pl.multiple_of(i * 256, 256), 256)
            feat_t[cols, pl.ds(col, R)] = jnp.transpose(src[:, cols])

    @pl.when(core == 0)
    def _():
        gather(0)

    @pl.when(core == 1)
    def _():
        gather(1)

    @pl.loop(0, E // 384)
    def _(i):
        cols = pl.ds(pl.multiple_of(i * 384, 384), 384)
        unit[:, cols] = dot(feat[...], w_ref[:, cols])

    @pl.loop(0, R // 32)
    def _(i):
        rows = pl.ds(pl.multiple_of(i * 32, 32), 32)
        e = unit[rows, :]
        inv = 1.0 / jnp.sqrt(jnp.sum(e * e, axis=1, keepdims=True) + EPS)
        u = e * inv
        unit[rows, :] = u
        length[rows, :] = inv
        img[rows, :] = u.astype(BF16)

    def slot(k):
        return img.at[pl.ds(k * R, R), :]

    @pl.when(core == 1)
    def _():
        send(1, slot(0), slot(1), (ex_s, 5), ex_r.at[5], near(1), lambda: slot(0))
        send(1, slot(0), slot(3), (ex_s, 6), ex_r.at[7], near(3), lambda: slot(0))

    @pl.when(core == 0)
    def _():
        send(0, slot(0), slot(1), (ex_s, 5), ex_r.at[5], near(1), lambda: slot(0))
        send(0, slot(0), slot(2), (ex_s, 6), ex_r.at[6], near(2), lambda: slot(0))

    text_norm(0)
    transpose(feat, 0)
    arrived(feat2, ex_s.at[4], ex_r.at[0])
    transpose(feat2, R)

    @pl.when(core == 0)
    def _():
        arrived(traw.at[1], ex_s.at[0], ex_r.at[1])
        arrived(traw.at[2], ex_s.at[0], ex_r.at[2])

    arrived(traw.at[3], ex_s.at[0], ex_r.at[3])
    for s in range(1, S):
        text_norm(s)

    factor = jnp.exp(jnp.full((1, R), nef_ref[0], F32))
    bias = bias_ref[0]

    def derivative(logit_dot, diagonal):
        logits = factor * logit_dot + bias
        if diagonal:
            same = lax.broadcasted_iota(jnp.int32, (R, R), 0) == lax.broadcasted_iota(jnp.int32, (R, R), 1)
            label = jnp.where(same, 1.0, -1.0).astype(F32)
            g = -factor * label / (1.0 + jnp.exp(label * logits))
        else:
            g = factor / (1.0 + jnp.exp(-logits))
        return g.astype(BF16)

    def back(grad, u, inv):
        return (grad - u * jnp.sum(u * grad, axis=1, keepdims=True)) * inv

    for s in range(S):
        pair[:, pl.ds(s * R, R)] = derivative(dot_nt(img[pl.ds(0, R), :], tlow[pl.ds(s * R, R), :]), s == 0)

    @pl.loop(0, R // 32)
    def _(i):
        rows = pl.ds(pl.multiple_of(i * 32, 32), 32)
        grad = dot(pair[rows, :], tlow[...])
        eg[rows, :] = back(grad, unit[rows, :], length[rows, :]).astype(BF16)

    @pl.when(core == 0)
    def _():
        part = pl.ds(COLS[1][0], COLS[1][1])
        send(0, eg.at[pl.ds(0, R), part], eg.at[pl.ds(R, R), part], (ex_s, 9), ex_r.at[9], me + 1, lambda: eg.at[pl.ds(0, R), pl.ds(COLS[1][0], COLS[1][1])])

    @pl.when(core == 1)
    def _():
        part = pl.ds(COLS[0][0], COLS[0][1])
        send(1, eg.at[pl.ds(0, R), part], eg.at[pl.ds(R, R), part], (ex_s, 9), ex_r.at[9], me - 1, lambda: eg.at[pl.ds(0, R), pl.ds(COLS[0][0], COLS[0][1])])

    @pl.loop(0, D // 384)
    def _(i):
        cols = pl.ds(pl.multiple_of(i * 384, 384), 384)
        gfeat[:, cols] = dot_nt(eg[pl.ds(0, R), :], w_ref[cols, :]).astype(BF16)

    cp_gf = pltpu.make_async_copy(gfeat, gf_hbm, out_sem.at[0])
    cp_gf.start()

    def text_forward():
        @pl.when(core == 0)
        def _():
            arrived(slot(1), ex_s.at[0], ex_r.at[5])
            send(0, slot(1), slot(2), (ex_s, 7), ex_r.at[6], near(1), lambda: slot(0))
            arrived(slot(2), ex_s.at[0], ex_r.at[6])
            send(0, slot(2), slot(3), (ex_s, 8), ex_r.at[7], near(1), lambda: slot(0))

        @pl.when(core == 1)
        def _():
            arrived(slot(1), ex_s.at[0], ex_r.at[5])
            arrived(slot(2), ex_s.at[0], ex_r.at[6])

        arrived(slot(3), ex_s.at[0], ex_r.at[7])

    def reduce_weight(c):
        c0, cw = COLS[c]
        count = [0]
        arrived(eg.at[pl.ds(R, R), pl.ds(c0, cw)], ex_s.at[0], ex_r.at[9])

        def product(j):
            rows = pl.ds(pl.multiple_of(lax.rem(y + j, NY) * YROWS, 8), YROWS)
            gpart[rows, pl.ds(0, cw)] = dot(feat_t[rows, :], eg[:, pl.ds(c0, cw)]).astype(BF16)

        def mine(dy, dz):
            return wblock(gpart, y + (dy + NY), z + (dz + NZ), 0, cw)

        def buf(i):
            return rbuf.at[i, :, pl.ds(0, cw)]

        def emit(src, i, dy, dz):
            send(c, src, buf(i), (rs_s, count[0]), rs_r.at[i], dev(dy, dz), lambda: buf(0))
            count[0] += 1

        def take(i):
            arrived(buf(i), rs_s.at[0], rs_r.at[i])
            return buf(i)[...].astype(F32)

        if c == 1:
            product(2)
            for i, k in enumerate(Z_ORDER + (0,)):
                emit(mine(2, k), k, 1 if i % 2 == 0 else -1, 0)
            product(1)
            product(3)
            product(0)
            for i, k in enumerate(Z_ORDER + (0,)):
                step = 1 if i % 2 == 0 else -1
                part = mine(step, k)
                other = mine(-step, k)
                emit(other, 8 + k if step == -1 else 16 + k, -step, 0)
                part[...] = (part[...].astype(F32) + take(k)).astype(BF16)
                emit(part, 8 + k if step == 1 else 16 + k, step, 0)
            for i, k in enumerate(Z_ORDER + (0,)):
                total = mine(0, k)[...].astype(F32) + take(8 + k) + take(16 + k)
                if k:
                    sbuf[k, :, pl.ds(0, cw)] = total.astype(BF16)
                    emit(sbuf.at[k, :, pl.ds(0, cw)], 24 + k, 0, k)
            for k in Z_ARRIVAL[1:]:
                total = total + take(24 + k)
        else:
            for j in range(NY):
                product(j)
            order = (2, 1, 3, 0)
            plus, minus = (2, 1), (3, 0)
            for j in order:
                emit(mine(j, 4), j if j in plus else 16 + j, 0, 1 if j in plus else -1)
            for h in (3, 2, 1):
                s = 3 - h
                for j in order:
                    for sign, base in ((1, 0), (-1, 16)):
                        part = mine(j, sign * h)
                        if s or j in (plus if sign == 1 else minus):
                            part[...] = (part[...].astype(F32) + take(base + 4 * s + j)).astype(BF16)
                        emit(part, base + 4 * (s + 1) + j, 0, sign)
            for j in order:
                total = mine(j, 0)[...].astype(F32) + take(12 + j) + take(28 + j)
                if j:
                    sbuf[j, :, pl.ds(0, cw)] = total.astype(BF16)
                    emit(sbuf.at[j, :, pl.ds(0, cw)], 32 + j, j, 0)
            for j in (1, 3, 2):
                total = total + take(32 + j)

        xrow[:, pl.ds(0, cw)] = total
        for k in range(ROW):
            xs[k, :, pl.ds(0, cw)] = xrow[pl.ds(SH * k, SH), pl.ds(0, cw)]
        for k in (4, 3, 5, 2, 6, 1, 7):
            send(
                c, xs.at[lax.rem(r + k, ROW), :, pl.ds(0, cw)], xr.at[r, :, pl.ds(0, cw)],
                (xg_s, k), xg_r.at[k], row_dev(k), lambda: xs.at[0, :, pl.ds(0, cw)],
            )
        xr[r, :, pl.ds(0, cw)] = xs[r, :, pl.ds(0, cw)]

    @pl.when(core == 0)
    def _():
        reduce_weight(0)

    @pl.when(core == 1)
    def _():
        reduce_weight(1)

    text_forward()
    for s in range(S):
        pair[:, pl.ds(s * R, R)] = derivative(dot_nt(tlow[pl.ds(0, R), :], img[pl.ds(s * R, R), :]), s == 0)

    @pl.loop(0, R // 32)
    def _(i):
        rows = pl.ds(pl.multiple_of(i * 32, 32), 32)
        grad = dot(pair[rows, :], img[...])
        inv = tlen[rows, :]
        gtext[rows, :] = back(grad, traw[0, rows, :].astype(F32) * inv, inv).astype(BF16)

    cp_gt = pltpu.make_async_copy(gtext, gt_hbm, out_sem.at[1])
    cp_gt.start()

    for k in range(1, ROW):
        source = lax.rem(r + (ROW - k), ROW)

        @pl.when(lax.rem(source, 2) == 1)
        def _():
            arrived(xr.at[source, :, pl.ds(0, COLS[1][1])], xg_s.at[k], xg_r.at[k])

        @pl.when(lax.rem(source, 2) == 0)
        def _():
            arrived(xr.at[source, :, pl.ds(0, COLS[0][1])], xg_s.at[k], xg_r.at[k])

    for c in range(2):
        c0, cw = COLS[c]
        total = xr[c, :, pl.ds(0, cw)]
        for k in range(1, NX):
            total = total + xr[2 * k + c, :, pl.ds(0, cw)]
        gout[:, pl.ds(c0, cw)] = total
    cp_gw = pltpu.make_async_copy(gout, gw_hbm, out_sem.at[2])
    cp_gw.start()

    for only, wait in pending:
        if only is None:
            wait()
    for c in range(2):

        @pl.when(core == c)
        def _():
            for only, wait in pending:
                if only == c:
                    wait()

    cp_gf.wait()
    cp_gt.wait()
    cp_gw.wait()


def on_device(image_features, head_weight, text_embeds, natural_exponent_factor, logit_bias):
    dma = pltpu.SemaphoreType.DMA
    anywhere = pl.BlockSpec(memory_space=pl.ANY)
    scalar = pl.BlockSpec(memory_space=pltpu.SMEM)
    return pl.pallas_call(
        kernel,
        out_shape=(
            jax.ShapeDtypeStruct((R, D), BF16),
            jax.ShapeDtypeStruct((R, E), BF16),
            jax.ShapeDtypeStruct((SH, E), F32),
        ),
        in_specs=[anywhere, anywhere, anywhere, scalar, scalar],
        out_specs=(anywhere, anywhere, anywhere),
        scratch_shapes=[
            pltpu.VMEM((D, E), BF16),
            pltpu.VMEM((R, D), BF16),
            pltpu.VMEM((R, D), BF16),
            pltpu.VMEM((D, 2 * R), BF16),
            pltpu.VMEM((R, E), F32),
            pltpu.VMEM((R, 1), F32),
            pltpu.VMEM((S * R, E), BF16),
            pltpu.VMEM((S, R, E), BF16),
            pltpu.VMEM((S * R, E), BF16),
            pltpu.VMEM((R, 1), F32),
            pltpu.VMEM((R, S * R), BF16),
            pltpu.VMEM((2 * R, E), BF16),
            pltpu.VMEM((R, D), BF16),
            pltpu.VMEM((R, E), BF16),
            pltpu.VMEM((D, W1), BF16),
            pltpu.VMEM((ROW, SH, E), BF16),
            pltpu.VMEM((BLK, E), F32),
            pltpu.VMEM((36, BLK, W1), BF16),
            pltpu.VMEM((8, BLK, W1), BF16),
            pltpu.VMEM((BLK, W1), F32),
            pltpu.VMEM((ROW, SH, W1), F32),
            pltpu.VMEM((ROW, SH, W1), F32),
            pltpu.VMEM((SH, E), F32),
            dma((3,)), dma((3,)),
            dma((ROW,)), dma((ROW,)),
            dma((32,)), dma((32,)),
            dma((32,)), dma((32,)),
            dma((10,)), dma((10,)),
            dma((40,)), dma((36,)),
            dma((ROW,)), dma((ROW,)),
        ],
        compiler_params=pltpu.CompilerParams(
            collective_id=0, has_side_effects=True, vmem_limit_bytes=56 * 1024 * 1024
        ),
    )(image_features, head_weight, text_embeds, natural_exponent_factor, logit_bias)


def solution(mesh):
    split = P("blk", None)
    return jax.shard_map(
        on_device,
        mesh=mesh,
        in_specs=(split, split, split, P(), P()),
        out_specs=(split, split, split),
        check_vma=False,
    )
```

time: 281 us -> 111 us (0.40)
  waiting for transfers between devices: 151 us -> 0 us
  Pallas kernels: 0 us -> 105 us
  starting transfers between devices: 43.3 us -> 0 us
  matrix products: 33.6 us -> 0 us
  local copies, waits for them, and re-layouts: 26.9 us -> 3.56 us
  between operations: 15.5 us -> 1.94 us
  other arithmetic: 8.36 us -> 0 us
    pallas_call x0 -> x1, Pallas kernels: none -> 105 us  [on_device(): pl.pallas_call(kernel, out_shape=(jax.ShapeDtypeStruct((R, D), BF16), jax...]
    all_gather x1 -> x0, waiting for transfers between devices: 87.6 us -> none  [on_device(): full_weight = lax.all_gather(head_weight, BLK, axis=0, tiled=True)]
    ppermute x6 -> x0, waiting for transfers between devices: 51.7 us -> none  [passed_along(): return lax.ppermute(block, axis, route)]
    dot_general x12 -> x0, matrix products: 33.6 us -> none  [the longest x4 11.3 us: on_device(): jnp.dot(mapping_matrix, current_neighbour_tile, preferred_element_type=jn...]
    ppermute x6 -> x0, starting transfers between devices: 31.7 us -> none  [passed_along(): return lax.ppermute(block, axis, route)]
    all_to_all x2 -> x0, starting transfers between devices: 11.6 us -> none  [the longest x1 6.96 us: sum_by_axis(): lax.all_to_all(own.astype(jnp.bfloat16), far, 0, 0, tiled=True)]
    all_to_all x2 -> x0, waiting for transfers between devices: 10.9 us -> none  [the longest x1 10.9 us: sum_by_axis(): lax.all_to_all(own.astype(jnp.bfloat16), far, 0, 0, tiled=True)]
    another operation x1 -> x0, local copies, waits for them, and re-layouts: 6.66 us -> none  [in_blocks(): return jnp.moveaxis(x.reshape(*before, peers, -1, *after), dim, 0)]
  transfers between devices with their start and end apart: 9 -> 0, of which waited for: 6 -> 0; matrix products, arithmetic and copies ran while one was open for 15% -> 0% of each run, Pallas kernels for 0% -> 0%
where the time goes in v1:
time: 111 us
  Pallas kernels  105 us (95%)
  local copies, waits for them, and re-layouts  3.56 us (3%)
  between operations  1.94 us (2%)
    pallas_call x1, Pallas kernels, on_device(): pl.pallas_call(kernel, out_shape=(jax.ShapeDtypeStruct((R, D), BF16), jax...  105 us
    unnamed x7, local copies, waits for them, and re-layouts  3.56 us

profile of v1, /device:TPU:1, one launch (start us, length us, event | category | flops | bytes accessed | tf_op | source)
XLA Modules:
  0.0 110.7 jit_solution(9411473663321801301)
XLA Ops:
  1.9 105.2 %shard_map.76 = (bf16[256,1536]{1,0:T(8,128)(2,1)}, bf16[256,1152]{1,0:T(8,128)(2,1)}, f32[6,1152]{1,0:T(8,128)}) custom-call(bf16[256,1536]{1,0:T(8,128)(2,1)} %feat_hbm.1, bf16[6,1152]{1,0:T(8,128)(2,1)} %w_hbm.1, bf16[256,1152]{1,0:T(8,128)(2,1)} %text_hbm.1, f32[1]{0:T(128)S(6)} %copy.11.nef_ref, f32[1]{0:T(128)S(6)} %copy.12.bias_ref), custom_call_target="tpu_custom_call" | custom-call | tf_op jit(solution)/shard_map/pallas_call | solution.py:473
  107.1 0.0 copy-start
  107.1 2.1 %copy.13 = bf16[256,1536]{1,0:T(8,128)(2,1)} copy(bf16[256,1536]{1,0:T(8,128)(2,1)} %get-tuple-element.6) | data formatting | bytes 1572864
  109.3 0.0 copy-done
  109.3 0.0 copy-start.1
  109.3 0.8 copy.14
  110.1 0.0 copy-done.1
  110.1 0.6 copy.15
Async XLA Ops:
  107.1 2.1 %copy-start = (bf16[256,1152]{1,0:T(8,128)(2,1)S(1)}, bf16[256,1152]{1,0:T(8,128)(2,1)}, u32[]{:S(2)}) copy-start(bf16[256,1152]{1,0:T(8,128)(2,1)} %get-tuple-element.7) | copy-start | bytes 1769476
  109.3 0.8 copy-start.1

commit v2 on v1

v2 whole, which is shorter than its diff:
```python
import jax
import jax.numpy as jnp
from jax import lax
from jax.experimental import pallas as pl
from jax.experimental.pallas import tpu as pltpu
from jax.sharding import PartitionSpec as P

MESH = pl.DeviceIdType.MESH
D, E, R, S = 1536, 1152, 256, 4
NY, NZ, NX = 4, 8, 4
N = NY * NZ * NX * 2
ROW = NX * 2
SH = D // N
BLK = SH * ROW
YROWS = BLK * NZ
W1 = 640
COLS = ((0, W1), (W1, E - W1))
Y_CORE = 0
EPS = 1e-06
TILES = ((0, 512), (512, 512), (1024, 128))
F32, BF16 = jnp.float32, jnp.bfloat16
Z_ORDER = (4, 3, 5, 2, 6, 1, 7)
Z_ARRIVAL = (0, 1, 7, 2, 6, 3, 5, 4)
ORDER_NT = (((1,), (1,)), ((), ()))


def dot(a, b):
    return jnp.dot(a, b, preferred_element_type=F32)


def dot_nt(a, b):
    return lax.dot_general(a, b, ORDER_NT, preferred_element_type=F32)


def kernel(
    feat_hbm, w_hbm, text_hbm, nef_ref, bias_ref,
    gfeat, gtext, gout,
    w_ref, feat, feat2, feat_t, unit, length, img, traw, tlow, tlen, pair, eg,
    gpart, xbuf, wrow, rbuf, sbuf, xrow, xs, xr, igrad,
    in_sem, xw_s, xw_r, ag_s, ag_r, dd_s, dd_r, ex_s, ex_r, rs_s, rs_r, xg_s, xg_r,
):
    me = lax.axis_index("blk")
    core = lax.rem(me, 2)
    r = lax.rem(me, ROW)
    z = lax.rem(lax.div(me, ROW), NZ)
    y = lax.div(me, ROW * NZ)
    pending = []

    def dev(dy=0, dz=0):
        return (lax.rem(y + (dy + NY) , NY) * NZ + lax.rem(z + (dz + NZ), NZ)) * ROW + r

    def row_dev(k):
        return me - r + lax.rem(r + k, ROW)

    def near(k):
        return lax.rem(me + (k + N), N)

    def remote(src, dst, ss, rs, to):
        return pltpu.make_async_remote_copy(
            src_ref=src, dst_ref=dst, send_sem=ss, recv_sem=rs, device_id=(to,), device_id_type=MESH
        )

    def send(only, src, dst, ss, rs, to, like=None):
        sems, i = ss
        remote(src, dst, sems.at[i], rs, to).start()

        def wait():
            ref = src if like is None else like()
            remote(ref, ref, sems.at[i], sems.at[i], near(1)).wait_send()

        pending.append((only, wait))

    def arrived(dst, ss, rs):
        remote(dst, dst, ss, rs, near(1)).wait_recv()

    def wblock(ref, yy, zz, c0, cw):
        start = pl.multiple_of(lax.rem(yy, NY) * YROWS + lax.rem(zz, NZ) * BLK, 8)
        return ref.at[pl.ds(start, BLK), pl.ds(c0, cw)]

    def transpose(src, col):
        if col:
            arrived(feat2, ex_s.at[4], ex_r.at[0])

        @pl.loop(0, D // 256)
        def _(i):
            cols = pl.ds(pl.multiple_of(i * 256, 256), 256)
            feat_t[cols, pl.ds(col, R)] = jnp.transpose(src[:, cols])

    def tslot(k):
        return tlow.at[pl.ds(k * R, R), :]

    def slot(k):
        return img.at[pl.ds(k * R, R), :]

    cp_w = pltpu.make_async_copy(w_hbm, xbuf.at[r], in_sem.at[0])
    cp_t = pltpu.make_async_copy(text_hbm, traw, in_sem.at[1])
    cp_f = pltpu.make_async_copy(feat_hbm, feat, in_sem.at[2])
    cp_w.start()
    cp_t.start()
    cp_f.start()

    with jax.named_scope("barrier"):
        barrier = pltpu.get_barrier_semaphore()
        peers = [row_dev(k) for k in range(1, ROW)] + [dev(dz=k) for k in range(1, NZ)]
        peers += [dev(dy=k) for k in range(1, NY)] + [near(k) for k in (-2, -1, 1, 2)]
        for peer in peers:
            pl.semaphore_signal(barrier, inc=1, device_id=(peer,), device_id_type=MESH)
        pl.semaphore_wait(barrier, len(peers))

    with jax.named_scope("w_row_send"):
        cp_w.wait()
        for k in (4, 3, 5, 2, 6, 1, 7):
            send(None, xbuf.at[r], xbuf.at[r], (xw_s, k), xw_r.at[k], row_dev(k), lambda: xbuf.at[0])

    with jax.named_scope("own_text"):
        cp_t.wait()

        @pl.loop(0, R // 32)
        def _(i):
            rows = pl.ds(pl.multiple_of(i * 32, 32), 32)
            t = traw[rows, :].astype(F32)
            inv = 1.0 / jnp.sqrt(jnp.sum(t * t, axis=1, keepdims=True) + EPS)
            tlow[rows, :] = (t * inv).astype(BF16)
            tlen[rows, :] = inv

        cp_f.wait()
        send(None, feat, feat2, (ex_s, 4), ex_r.at[0], me + 1 - 2 * core)
        transpose(feat, 0)

    with jax.named_scope("w_row"):
        for k in range(1, ROW):
            arrived(xbuf.at[lax.rem(r + (ROW - k), ROW)], xw_s.at[k], xw_r.at[k])
        for k in range(ROW):
            wrow[pl.ds(SH * k, SH), :] = xbuf[k].astype(F32)
        own = pl.multiple_of(y * YROWS + z * BLK, 8)
        w_ref[pl.ds(own, BLK), :] = wrow[...].astype(BF16)

    with jax.named_scope("text_send"):
        @pl.when(core == 0)
        def _():
            send(0, tslot(0), tslot(1), (ex_s, 0), ex_r.at[1], near(-1), lambda: tslot(0))

        @pl.when(core == 1)
        def _():
            send(1, tslot(0), tslot(1), (ex_s, 0), ex_r.at[1], near(-1), lambda: tslot(0))
            send(1, tslot(0), tslot(2), (ex_s, 1), ex_r.at[2], near(-2), lambda: tslot(0))


    def gather(c):
        c0, cw = COLS[c]
        sibling = me + (1 - 2 * c)
        count = [0]
        like = lambda: w_ref.at[pl.ds(0, BLK), pl.ds(c0, cw)]

        def put(j, k, dy, dz):
            part = wblock(w_ref, y + (NY - j), z + (NZ - k), c0, cw)
            idx = ((j + dy) % NY) * NZ + (k + dz) % NZ
            send(c, part, part, (ag_s, count[0]), ag_r.at[idx], dev(dy, dz), like)
            count[0] += 1

        def share(j, k):
            part = wblock(w_ref, y + (NY - j), z + (NZ - k), c0, cw)
            send(c, part, part, (dd_s, j * NZ + k), dd_r.at[j * NZ + k], sibling, like)

        def got(j, k):
            part = wblock(w_ref, y + (NY - j), z + (NZ - k), c0, cw)
            arrived(part, ag_s.at[0], ag_r.at[j * NZ + k])
            return part

        if c == Y_CORE:
            for k in Z_ARRIVAL[1:]:
                put(0, 0, 0, k)
            transpose(feat2, R)

            def stage1(i):
                k = Z_ARRIVAL[i]
                if k:
                    got(0, k)
                put(0, k, 1, 0)
                put(0, k, -1, 0)
                if k:
                    share(0, k)

            def stage2(i):
                k = Z_ARRIVAL[i]
                got(1, k)
                if i % 2 == 0:
                    put(1, k, 1, 0)
                share(1, k)
                got(3, k)
                if i % 2 == 1:
                    put(3, k, -1, 0)
                share(3, k)

            def stage3(i):
                k = Z_ARRIVAL[i]
                got(2, k)
                share(2, k)

            for i in range(NZ + 4):
                if i < NZ:
                    stage1(i)
                if 2 <= i < NZ + 2:
                    stage2(i - 2)
                if 4 <= i:
                    stage3(i - 4)
        else:
            for j in (1, 3, 2):
                put(0, 0, j, 0)
            for j in (0, 1, 3, 2):
                if j:
                    got(j, 0)
                put(j, 0, 0, 1)
                put(j, 0, 0, -1)
                if j == 0:
                    transpose(feat2, R)
                if j:
                    share(j, 0)
            for h in (1, 2, 3):
                for j in (0, 1, 3, 2):
                    got(j, h)
                    if h < 3 or j in (0, 3):
                        put(j, h, 0, 1)
                    share(j, h)
                    got(j, NZ - h)
                    if h < 3 or j in (1, 2):
                        put(j, NZ - h, 0, -1)
                    share(j, NZ - h)
            for j in (0, 1, 3, 2):
                got(j, 4)
                share(j, 4)
            arrived(tslot(1), ex_s.at[0], ex_r.at[1])
            send(1, tslot(1), tslot(3), (ex_s, 2), ex_r.at[3], near(-2), lambda: tslot(0))
            send(1, tslot(1), tslot(2), (ex_s, 3), ex_r.at[2], near(-1), lambda: tslot(0))
            arrived(tslot(2), ex_s.at[0], ex_r.at[2])
            send(1, tslot(2), tslot(3), (ex_s, 10), ex_r.at[3], near(-1), lambda: tslot(0))
        o0, ow = COLS[1 - c]
        for j in range(NY):
            for k in range(NZ):
                if j or k:
                    part = wblock(w_ref, y + (NY - j), z + (NZ - k), o0, ow)
                    arrived(part, dd_s.at[0], dd_r.at[j * NZ + k])

    with jax.named_scope("gather"):
        @pl.when(core == 0)
        def _():
            gather(0)

        @pl.when(core == 1)
        def _():
            gather(1)

    with jax.named_scope("embed"):
        for c0, cw in TILES:
            unit[:, pl.ds(c0, cw)] = dot(feat[...], w_ref[:, pl.ds(c0, cw)])

        @pl.loop(0, R // 32)
        def _(i):
            rows = pl.ds(pl.multiple_of(i * 32, 32), 32)
            e = unit[rows, :]
            inv = 1.0 / jnp.sqrt(jnp.sum(e * e, axis=1, keepdims=True) + EPS)
            u = e * inv
            unit[rows, :] = u
            length[rows, :] = inv
            img[rows, :] = u.astype(BF16)

    with jax.named_scope("image_send"):
        @pl.when(core == 1)
        def _():
            send(1, slot(0), slot(1), (ex_s, 5), ex_r.at[5], near(1), lambda: slot(0))

        @pl.when(core == 0)
        def _():
            send(0, slot(0), slot(1), (ex_s, 5), ex_r.at[5], near(1), lambda: slot(0))
            send(0, slot(0), slot(2), (ex_s, 6), ex_r.at[6], near(2), lambda: slot(0))

    factor = jnp.exp(jnp.full((1, R), nef_ref[0], F32))
    bias = bias_ref[0]

    def derivative(logit_dot, diagonal):
        logits = factor * logit_dot + bias
        if diagonal:
            same = lax.broadcasted_iota(jnp.int32, (R, R), 0) == lax.broadcasted_iota(jnp.int32, (R, R), 1)
            label = jnp.where(same, 1.0, -1.0).astype(F32)
            g = -factor * label / (1.0 + jnp.exp(label * logits))
        else:
            g = factor / (1.0 + jnp.exp(-logits))
        return g.astype(BF16)

    def back(grad, u, inv):
        return (grad - u * jnp.sum(u * grad, axis=1, keepdims=True)) * inv

    with jax.named_scope("image_side"):
        for s in range(S):
            if s == 1:

                @pl.when(core == 0)
                def _():
                    arrived(tslot(1), ex_s.at[0], ex_r.at[1])
                    arrived(tslot(2), ex_s.at[0], ex_r.at[2])

            if s == 3:
                with jax.named_scope("text_wait"):
                    arrived(tslot(3), ex_s.at[0], ex_r.at[3])
            pair[:, pl.ds(s * R, R)] = derivative(dot_nt(img[pl.ds(0, R), :], tlow[pl.ds(s * R, R), :]), s == 0)
        for c0, cw in TILES:
            igrad[:, pl.ds(c0, cw)] = dot(pair[...], tlow[:, pl.ds(c0, cw)])

        @pl.loop(0, R // 32)
        def _(i):
            rows = pl.ds(pl.multiple_of(i * 32, 32), 32)
            eg[rows, :] = back(igrad[rows, :], unit[rows, :], length[rows, :]).astype(BF16)

    with jax.named_scope("eg_send"):
        @pl.when(core == 0)
        def _():
            part = pl.ds(COLS[1][0], COLS[1][1])
            send(0, eg.at[pl.ds(0, R), part], eg.at[pl.ds(R, R), part], (ex_s, 9), ex_r.at[9], me + 1, lambda: eg.at[pl.ds(0, R), pl.ds(COLS[1][0], COLS[1][1])])

        @pl.when(core == 1)
        def _():
            part = pl.ds(COLS[0][0], COLS[0][1])
            send(1, eg.at[pl.ds(0, R), part], eg.at[pl.ds(R, R), part], (ex_s, 9), ex_r.at[9], me - 1, lambda: eg.at[pl.ds(0, R), pl.ds(COLS[0][0], COLS[0][1])])

    with jax.named_scope("feat_grad"):
        @pl.loop(0, D // 512)
        def _(i):
            cols = pl.ds(pl.multiple_of(i * 512, 512), 512)
            gfeat[:, cols] = dot_nt(eg[pl.ds(0, R), :], w_ref[cols, :]).astype(BF16)


    def reduce_weight(c):
        c0, cw = COLS[c]
        count = [0]
        arrived(eg.at[pl.ds(R, R), pl.ds(c0, cw)], ex_s.at[0], ex_r.at[9])

        def product(j):
            rows = pl.ds(pl.multiple_of(lax.rem(y + j, NY) * YROWS, 8), YROWS)
            gpart[rows, pl.ds(0, cw)] = dot(feat_t[rows, :], eg[:, pl.ds(c0, cw)]).astype(BF16)

        def mine(dy, dz):
            return wblock(gpart, y + (dy + NY), z + (dz + NZ), 0, cw)

        def buf(i):
            return rbuf.at[i, :, pl.ds(0, cw)]

        def emit(src, i, dy, dz):
            send(c, src, buf(i), (rs_s, count[0]), rs_r.at[i], dev(dy, dz), lambda: buf(0))
            count[0] += 1

        def take(i):
            arrived(buf(i), rs_s.at[0], rs_r.at[i])
            return buf(i)[...].astype(F32)

        if c == Y_CORE:
            product(2)
            for i, k in enumerate(Z_ORDER + (0,)):
                emit(mine(2, k), k, 1 if i % 2 == 0 else -1, 0)
            product(1)
            product(3)
            product(0)
            for i, k in enumerate(Z_ORDER + (0,)):
                step = 1 if i % 2 == 0 else -1
                part = mine(step, k)
                other = mine(-step, k)
                emit(other, 8 + k if step == -1 else 16 + k, -step, 0)
                part[...] = (part[...].astype(F32) + take(k)).astype(BF16)
                emit(part, 8 + k if step == 1 else 16 + k, step, 0)
            for i, k in enumerate(Z_ORDER + (0,)):
                total = mine(0, k)[...].astype(F32) + take(8 + k) + take(16 + k)
                if k:
                    sbuf[k, :, pl.ds(0, cw)] = total.astype(BF16)
                    emit(sbuf.at[k, :, pl.ds(0, cw)], 24 + k, 0, k)
            arrived(slot(1), ex_s.at[0], ex_r.at[5])
            send(0, slot(1), slot(3), (ex_s, 7), ex_r.at[7], near(2), lambda: slot(0))
            send(0, slot(1), slot(2), (ex_s, 8), ex_r.at[6], near(1), lambda: slot(0))
            arrived(slot(2), ex_s.at[0], ex_r.at[6])
            send(0, slot(2), slot(3), (ex_s, 11), ex_r.at[7], near(1), lambda: slot(0))
            for k in Z_ARRIVAL[1:]:
                total = total + take(24 + k)
        else:
            for j in range(NY):
                product(j)
            order = (2, 1, 3, 0)
            plus, minus = (2, 1), (3, 0)
            for j in order:
                emit(mine(j, 4), j if j in plus else 16 + j, 0, 1 if j in plus else -1)
            for h in (3, 2, 1):
                s = 3 - h
                for j in order:
                    for sign, base in ((1, 0), (-1, 16)):
                        part = mine(j, sign * h)
                        if s or j in (plus if sign == 1 else minus):
                            part[...] = (part[...].astype(F32) + take(base + 4 * s + j)).astype(BF16)
                        emit(part, base + 4 * (s + 1) + j, 0, sign)
            for j in order:
                total = mine(j, 0)[...].astype(F32) + take(12 + j) + take(28 + j)
                if j:
                    sbuf[j, :, pl.ds(0, cw)] = total.astype(BF16)
                    emit(sbuf.at[j, :, pl.ds(0, cw)], 32 + j, j, 0)
            for j in (1, 3, 2):
                total = total + take(32 + j)

        xrow[:, pl.ds(0, cw)] = total
        for k in range(ROW):
            xs[k, :, pl.ds(0, cw)] = xrow[pl.ds(SH * k, SH), pl.ds(0, cw)]
        for k in (4, 3, 5, 2, 6, 1, 7):
            send(
                c, xs.at[lax.rem(r + k, ROW), :, pl.ds(0, cw)], xr.at[r, :, pl.ds(0, cw)],
                (xg_s, k), xg_r.at[k], row_dev(k), lambda: xs.at[0, :, pl.ds(0, cw)],
            )
        xr[r, :, pl.ds(0, cw)] = xs[r, :, pl.ds(0, cw)]

    with jax.named_scope("reduce"):
        @pl.when(core == 0)
        def _():
            reduce_weight(0)

        @pl.when(core == 1)
        def _():
            reduce_weight(1)

    with jax.named_scope("image_wait"):
        @pl.when(core == 1)
        def _():
            arrived(slot(1), ex_s.at[0], ex_r.at[5])
            arrived(slot(2), ex_s.at[0], ex_r.at[6])

        arrived(slot(3), ex_s.at[0], ex_r.at[7])
    with jax.named_scope("text_side"):
        for s in range(S):
            pair[:, pl.ds(s * R, R)] = derivative(dot_nt(tlow[pl.ds(0, R), :], img[pl.ds(s * R, R), :]), s == 0)
        for c0, cw in TILES:
            igrad[:, pl.ds(c0, cw)] = dot(pair[...], img[:, pl.ds(c0, cw)])

        @pl.loop(0, R // 32)
        def _(i):
            rows = pl.ds(pl.multiple_of(i * 32, 32), 32)
            inv = tlen[rows, :]
            gtext[rows, :] = back(igrad[rows, :], traw[rows, :].astype(F32) * inv, inv).astype(BF16)

    with jax.named_scope("final"):
        for k in range(1, ROW):
            source = lax.rem(r + (ROW - k), ROW)

            @pl.when(lax.rem(source, 2) == 1)
            def _():
                arrived(xr.at[source, :, pl.ds(0, COLS[1][1])], xg_s.at[k], xg_r.at[k])

            @pl.when(lax.rem(source, 2) == 0)
            def _():
                arrived(xr.at[source, :, pl.ds(0, COLS[0][1])], xg_s.at[k], xg_r.at[k])

        for c in range(2):
            c0, cw = COLS[c]
            total = xr[c, :, pl.ds(0, cw)]
            for k in range(1, NX):
                total = total + xr[2 * k + c, :, pl.ds(0, cw)]
            gout[:, pl.ds(c0, cw)] = total

    with jax.named_scope("drain"):
        for only, wait in pending:
            if only is None:
                wait()
        for c in range(2):

            @pl.when(core == c)
            def _():
                for only, wait in pending:
                    if only == c:
                        wait()


def on_device(image_features, head_weight, text_embeds, natural_exponent_factor, logit_bias):
    dma = pltpu.SemaphoreType.DMA
    anywhere = pl.BlockSpec(memory_space=pl.ANY)
    local = pl.BlockSpec(memory_space=pltpu.VMEM)
    scalar = pl.BlockSpec(memory_space=pltpu.SMEM)
    return pl.pallas_call(
        kernel,
        out_shape=(
            jax.ShapeDtypeStruct((R, D), BF16),
            jax.ShapeDtypeStruct((R, E), BF16),
            jax.ShapeDtypeStruct((SH, E), F32),
        ),
        in_specs=[anywhere, anywhere, anywhere, scalar, scalar],
        out_specs=(local, local, local),
        scratch_shapes=[
            pltpu.VMEM((D, E), BF16),
            pltpu.VMEM((R, D), BF16),
            pltpu.VMEM((R, D), BF16),
            pltpu.VMEM((D, 2 * R), BF16),
            pltpu.VMEM((R, E), F32),
            pltpu.VMEM((R, 1), F32),
            pltpu.VMEM((S * R, E), BF16),
            pltpu.VMEM((R, E), BF16),
            pltpu.VMEM((S * R, E), BF16),
            pltpu.VMEM((R, 1), F32),
            pltpu.VMEM((R, S * R), BF16),
            pltpu.VMEM((2 * R, E), BF16),
            pltpu.VMEM((D, W1), BF16),
            pltpu.VMEM((ROW, SH, E), BF16),
            pltpu.VMEM((BLK, E), F32),
            pltpu.VMEM((36, BLK, W1), BF16),
            pltpu.VMEM((8, BLK, W1), BF16),
            pltpu.VMEM((BLK, W1), F32),
            pltpu.VMEM((ROW, SH, W1), F32),
            pltpu.VMEM((ROW, SH, W1), F32),
            pltpu.VMEM((R, E), F32),
            dma((3,)),
            dma((ROW,)), dma((ROW,)),
            dma((32,)), dma((32,)),
            dma((32,)), dma((32,)),
            dma((12,)), dma((10,)),
            dma((40,)), dma((36,)),
            dma((ROW,)), dma((ROW,)),
        ],
        compiler_params=pltpu.CompilerParams(
            collective_id=0, has_side_effects=True, vmem_limit_bytes=32 * 1024 * 1024
        ),
    )(image_features, head_weight, text_embeds, natural_exponent_factor, logit_bias)


def solution(mesh):
    split = P("blk", None)
    return jax.shard_map(
        on_device,
        mesh=mesh,
        in_specs=(split, split, split, P(), P()),
        out_specs=(split, split, split),
        check_vma=False,
    )
```

time: 111 us -> 95.5 us (0.86); the launches traced: 111 us -> 93.8 us
  Pallas kernels: 105 us -> 86.6 us
  local copies, waits for them, and re-layouts: 3.56 us -> 5.22 us
    pallas_call x1, Pallas kernels: 105 us -> 86.6 us  [on_device(): pl.pallas_call(kernel, out_shape=(jax.ShapeDtypeStruct((R, D), BF16), jax...]
    unnamed x7 -> x9, local copies, waits for them, and re-layouts: 3.56 us -> 5.22 us
where the time goes in v2:
time: 95.5 us; the launch traced here: 93.8 us
  Pallas kernels  86.6 us (91%)
  local copies, waits for them, and re-layouts  5.22 us (5%)
  between operations  1.94 us (2%)
    pallas_call x1, Pallas kernels, on_device(): pl.pallas_call(kernel, out_shape=(jax.ShapeDtypeStruct((R, D), BF16), jax...  86.6 us
    unnamed x9, local copies, waits for them, and re-layouts  5.22 us

profile of v2, /device:TPU:1, one launch (start us, length us, event | category | flops | bytes accessed | tf_op | source)
XLA Modules:
  0.0 93.8 jit_solution(9775086281119033051)
XLA Ops:
  1.9 0.0 copy-start
  1.9 1.1 %copy-done = bf16[256,1536]{1,0:T(8,128)(2,1)S(1)} copy-done((bf16[256,1536]{1,0:T(8,128)(2,1)S(1)}, bf16[256,1536]{1,0:T(8,128)(2,1)}, u32[]{:S(2)}) %copy-start) | copy-done | bytes 786456
  3.1 0.0 copy-start.1
  3.1 1.1 %copy-done.1 = bf16[256,1152]{1,0:T(8,128)(2,1)S(1)} copy-done((bf16[256,1152]{1,0:T(8,128)(2,1)S(1)}, bf16[256,1152]{1,0:T(8,128)(2,1)}, u32[]{:S(2)}) %copy-start.1) | copy-done | bytes 589848
  4.1 0.0 copy-start.2
  4.1 0.7 copy-done.2
  4.8 86.6 %shard_map.76 = (bf16[256,1536]{1,0:T(8,128)(2,1)S(1)}, bf16[256,1152]{1,0:T(8,128)(2,1)S(1)}, f32[6,1152]{1,0:T(8,128)S(1)}) custom-call(bf16[256,1536]{1,0:T(8,128)(2,1)S(1)} %copy-done, bf16[6,1152]{1,0:T(8,128)(2,1)S(1)} %copy-done.2, bf16[256,1152]{1,0:T(8,128)(2,1)S(1)} %copy-done.1, f32[1]{0:T(128)S(6)} %copy.11.nef_ref, f32[1]{0:T(128)S(6)} %copy.12.bias_ref), custom_call_target="tpu_custom_call" | custom-call | tf_op jit(solution)/shard_map/pallas_call | solution.py:479
  91.4 0.9 copy.13
  92.3 0.8 copy.14
  93.1 0.6 copy.15
Async XLA Ops:
  1.9 1.1 %copy-start = (bf16[256,1536]{1,0:T(8,128)(2,1)S(1)}, bf16[256,1536]{1,0:T(8,128)(2,1)}, u32[]{:S(2)}) copy-start(bf16[256,1536]{1,0:T(8,128)(2,1)} %feat_hbm.1) | copy-start | bytes 2359300
  3.1 1.1 %copy-start.1 = (bf16[256,1152]{1,0:T(8,128)(2,1)S(1)}, bf16[256,1152]{1,0:T(8,128)(2,1)}, u32[]{:S(2)}) copy-start(bf16[256,1152]{1,0:T(8,128)(2,1)} %text_hbm.1) | copy-start | bytes 1769476
  4.1 0.7 copy-start.2

commit v3 on v2

--- a/solution.py
+++ b/solution.py
@@ -36,7 +36,7 @@
     feat_hbm, w_hbm, text_hbm, nef_ref, bias_ref,
     gfeat, gtext, gout,
     w_ref, feat, feat2, feat_t, unit, length, img, traw, tlow, tlen, pair, eg,
-    gpart, xbuf, wrow, rbuf, sbuf, xrow, xs, xr, igrad,
+    gpart, xbuf, wrow, rbuf, sbuf, xrow, xs, xr, igrad, cross,
     in_sem, xw_s, xw_r, ag_s, ag_r, dd_s, dd_r, ex_s, ex_r, rs_s, rs_r, xg_s, xg_r,
 ):
     me = lax.axis_index("blk")
@@ -79,7 +79,7 @@
 
     def transpose(src, col):
         if col:
-            arrived(feat2, ex_s.at[4], ex_r.at[0])
+            arrived(feat2, ex_s.at[12], ex_r.at[0])
 
         @pl.loop(0, D // 256)
         def _(i):
@@ -102,7 +102,7 @@
     with jax.named_scope("barrier"):
         barrier = pltpu.get_barrier_semaphore()
         peers = [row_dev(k) for k in range(1, ROW)] + [dev(dz=k) for k in range(1, NZ)]
-        peers += [dev(dy=k) for k in range(1, NY)] + [near(k) for k in (-2, -1, 1, 2)]
+        peers += [dev(dy=k) for k in range(1, NY)] + [near(k) for k in (-ROW, -3, -2, -1, 1, 2, 3, ROW)]
         for peer in peers:
             pl.semaphore_signal(barrier, inc=1, device_id=(peer,), device_id_type=MESH)
         pl.semaphore_wait(barrier, len(peers))
@@ -124,8 +124,29 @@
             tlen[rows, :] = inv
 
         cp_f.wait()
-        send(None, feat, feat2, (ex_s, 4), ex_r.at[0], me + 1 - 2 * core)
+        send(None, feat, feat2, (ex_s, 12), ex_r.at[0], me + 1 - 2 * core)
         transpose(feat, 0)
+
+    with jax.named_scope("text_send"):
+        @pl.when(core == 0)
+        def _():
+            send(0, tslot(0), tslot(1), (ex_s, 0), ex_r.at[1], near(-1), lambda: tslot(0))
+
+        @pl.when((core == 0) & (r != 0))
+        def _():
+            send("t3", tslot(0), tslot(3), (ex_s, 1), ex_r.at[3], near(-3), lambda: tslot(0))
+
+        @pl.when(core == 1)
+        def _():
+            send(1, tslot(0), tslot(1), (ex_s, 0), ex_r.at[1], near(-1), lambda: tslot(0))
+
+        @pl.when((core == 1) & (r != 1))
+        def _():
+            send("t2", tslot(0), tslot(2), (ex_s, 1), ex_r.at[2], near(-2), lambda: tslot(0))
+
+        @pl.when(r == 1)
+        def _():
+            send("t1", tslot(0), cross, (ex_s, 1), ex_r.at[8], near(6), lambda: tslot(0))
 
     with jax.named_scope("w_row"):
         for k in range(1, ROW):
@@ -134,17 +155,6 @@
             wrow[pl.ds(SH * k, SH), :] = xbuf[k].astype(F32)
         own = pl.multiple_of(y * YROWS + z * BLK, 8)
         w_ref[pl.ds(own, BLK), :] = wrow[...].astype(BF16)
-
-    with jax.named_scope("text_send"):
-        @pl.when(core == 0)
-        def _():
-            send(0, tslot(0), tslot(1), (ex_s, 0), ex_r.at[1], near(-1), lambda: tslot(0))
-
-        @pl.when(core == 1)
-        def _():
-            send(1, tslot(0), tslot(1), (ex_s, 0), ex_r.at[1], near(-1), lambda: tslot(0))
-            send(1, tslot(0), tslot(2), (ex_s, 1), ex_r.at[2], near(-2), lambda: tslot(0))
-
 
     def gather(c):
         c0, cw = COLS[c]
@@ -226,12 +236,24 @@
                     if h < 3 or j in (1, 2):
                         put(j, NZ - h, 0, -1)
                     share(j, NZ - h)
+                if h == 2:
+
+                    @pl.when(r == ROW - 1)
+                    def _():
+                        arrived(cross, ex_s.at[0], ex_r.at[8])
+                        send("t7", cross, tslot(2), (ex_s, 2), ex_r.at[2], near(-ROW), lambda: tslot(0))
+
+                if h == 3:
+                    arrived(tslot(1), ex_s.at[0], ex_r.at[1])
+                    send(1, tslot(1), tslot(2), (ex_s, 3), ex_r.at[2], near(-1), lambda: tslot(0))
+
+                    @pl.when(r == ROW - 1)
+                    def _():
+                        send("t7", tslot(1), tslot(3), (ex_s, 4), ex_r.at[3], near(-2), lambda: tslot(0))
+
             for j in (0, 1, 3, 2):
                 got(j, 4)
                 share(j, 4)
-            arrived(tslot(1), ex_s.at[0], ex_r.at[1])
-            send(1, tslot(1), tslot(3), (ex_s, 2), ex_r.at[3], near(-2), lambda: tslot(0))
-            send(1, tslot(1), tslot(2), (ex_s, 3), ex_r.at[2], near(-1), lambda: tslot(0))
             arrived(tslot(2), ex_s.at[0], ex_r.at[2])
             send(1, tslot(2), tslot(3), (ex_s, 10), ex_r.at[3], near(-1), lambda: tslot(0))
         o0, ow = COLS[1 - c]
@@ -269,10 +291,21 @@
         def _():
             send(1, slot(0), slot(1), (ex_s, 5), ex_r.at[5], near(1), lambda: slot(0))
 
+        @pl.when((core == 1) & (r != ROW - 1))
+        def _():
+            send("i3", slot(0), slot(3), (ex_s, 6), ex_r.at[7], near(3), lambda: slot(0))
+
         @pl.when(core == 0)
         def _():
             send(0, slot(0), slot(1), (ex_s, 5), ex_r.at[5], near(1), lambda: slot(0))
-            send(0, slot(0), slot(2), (ex_s, 6), ex_r.at[6], near(2), lambda: slot(0))
+
+        @pl.when((core == 0) & (r != ROW - 2))
+        def _():
+            send("i2", slot(0), slot(2), (ex_s, 6), ex_r.at[6], near(2), lambda: slot(0))
+
+        @pl.when(r == ROW - 2)
+        def _():
+            send("i6", slot(0), cross, (ex_s, 6), ex_r.at[9], near(-6), lambda: slot(0))
 
     factor = jnp.exp(jnp.full((1, R), nef_ref[0], F32))
     bias = bias_ref[0]
@@ -315,12 +348,12 @@
         @pl.when(core == 0)
         def _():
             part = pl.ds(COLS[1][0], COLS[1][1])
-            send(0, eg.at[pl.ds(0, R), part], eg.at[pl.ds(R, R), part], (ex_s, 9), ex_r.at[9], me + 1, lambda: eg.at[pl.ds(0, R), pl.ds(COLS[1][0], COLS[1][1])])
+            send(0, eg.at[pl.ds(0, R), part], eg.at[pl.ds(R, R), part], (ex_s, 9), ex_r.at[10], me + 1, lambda: eg.at[pl.ds(0, R), pl.ds(COLS[1][0], COLS[1][1])])
 
         @pl.when(core == 1)
         def _():
             part = pl.ds(COLS[0][0], COLS[0][1])
-            send(1, eg.at[pl.ds(0, R), part], eg.at[pl.ds(R, R), part], (ex_s, 9), ex_r.at[9], me - 1, lambda: eg.at[pl.ds(0, R), pl.ds(COLS[0][0], COLS[0][1])])
+            send(1, eg.at[pl.ds(0, R), part], eg.at[pl.ds(R, R), part], (ex_s, 9), ex_r.at[10], me - 1, lambda: eg.at[pl.ds(0, R), pl.ds(COLS[0][0], COLS[0][1])])
 
     with jax.named_scope("feat_grad"):
         @pl.loop(0, D // 512)
@@ -332,7 +365,7 @@
     def reduce_weight(c):
         c0, cw = COLS[c]
         count = [0]
-        arrived(eg.at[pl.ds(R, R), pl.ds(c0, cw)], ex_s.at[0], ex_r.at[9])
+        arrived(eg.at[pl.ds(R, R), pl.ds(c0, cw)], ex_s.at[0], ex_r.at[10])
 
         def product(j):
             rows = pl.ds(pl.multiple_of(lax.rem(y + j, NY) * YROWS, 8), YROWS)
@@ -366,14 +399,20 @@
                 emit(other, 8 + k if step == -1 else 16 + k, -step, 0)
                 part[...] = (part[...].astype(F32) + take(k)).astype(BF16)
                 emit(part, 8 + k if step == 1 else 16 + k, step, 0)
+            arrived(slot(1), ex_s.at[0], ex_r.at[5])
+            send(0, slot(1), slot(2), (ex_s, 8), ex_r.at[6], near(1), lambda: slot(0))
+
+            @pl.when(r == 0)
+            def _():
+                send("i0", slot(1), slot(3), (ex_s, 7), ex_r.at[7], near(2), lambda: slot(0))
+                arrived(cross, ex_s.at[0], ex_r.at[9])
+                send("i0", cross, slot(2), (ex_s, 13), ex_r.at[6], near(ROW), lambda: slot(0))
+
             for i, k in enumerate(Z_ORDER + (0,)):
                 total = mine(0, k)[...].astype(F32) + take(8 + k) + take(16 + k)
                 if k:
                     sbuf[k, :, pl.ds(0, cw)] = total.astype(BF16)
                     emit(sbuf.at[k, :, pl.ds(0, cw)], 24 + k, 0, k)
-            arrived(slot(1), ex_s.at[0], ex_r.at[5])
-            send(0, slot(1), slot(3), (ex_s, 7), ex_r.at[7], near(2), lambda: slot(0))
-            send(0, slot(1), slot(2), (ex_s, 8), ex_r.at[6], near(1), lambda: slot(0))
             arrived(slot(2), ex_s.at[0], ex_r.at[6])
             send(0, slot(2), slot(3), (ex_s, 11), ex_r.at[7], near(1), lambda: slot(0))
             for k in Z_ARRIVAL[1:]:
@@ -462,28 +501,41 @@
         for only, wait in pending:
             if only is None:
                 wait()
-        for c in range(2):
-
-            @pl.when(core == c)
+        groups = {
+            0: core == 0, 1: core == 1, "t1": r == 1, "t7": r == ROW - 1, "i6": r == ROW - 2, "i0": r == 0,
+            "t3": (core == 0) & (r != 0), "t2": (core == 1) & (r != 1),
+            "i3": (core == 1) & (r != ROW - 1), "i2": (core == 0) & (r != ROW - 2),
+        }
+        for group, inside in groups.items():
+
+            @pl.when(inside)
             def _():
                 for only, wait in pending:
-                    if only == c:
+                    if only == group:
                         wait()
+
+
+def put_out(gf, gt, gw, gf_out, gt_out, gw_out, sem):
+    copies = [pltpu.make_async_copy(a, b, sem.at[i]) for i, (a, b) in enumerate(((gf, gf_out), (gt, gt_out), (gw, gw_out)))]
+    for copy in copies:
+        copy.start()
+    for copy in copies:
+        copy.wait()
 
 
 def on_device(image_features, head_weight, text_embeds, natural_exponent_factor, logit_bias):
     dma = pltpu.SemaphoreType.DMA
-    anywhere = pl.BlockSpec(memory_space=pl.ANY)
+    hbm = pl.BlockSpec(memory_space=pltpu.HBM)
     local = pl.BlockSpec(memory_space=pltpu.VMEM)
     scalar = pl.BlockSpec(memory_space=pltpu.SMEM)
-    return pl.pallas_call(
+    results = pl.pallas_call(
         kernel,
         out_shape=(
             jax.ShapeDtypeStruct((R, D), BF16),
             jax.ShapeDtypeStruct((R, E), BF16),
             jax.ShapeDtypeStruct((SH, E), F32),
         ),
-        in_specs=[anywhere, anywhere, anywhere, scalar, scalar],
+        in_specs=[hbm, hbm, hbm, scalar, scalar],
         out_specs=(local, local, local),
         scratch_shapes=[
             pltpu.VMEM((D, E), BF16),
@@ -507,11 +559,12 @@
             pltpu.VMEM((ROW, SH, W1), F32),
             pltpu.VMEM((ROW, SH, W1), F32),
             pltpu.VMEM((R, E), F32),
+            pltpu.VMEM((R, E), BF16),
             dma((3,)),
             dma((ROW,)), dma((ROW,)),
             dma((32,)), dma((32,)),
             dma((32,)), dma((32,)),
-            dma((12,)), dma((10,)),
+            dma((14,)), dma((11,)),
             dma((40,)), dma((36,)),
             dma((ROW,)), dma((ROW,)),
         ],
@@ -519,6 +572,14 @@
             collective_id=0, has_side_effects=True, vmem_limit_bytes=32 * 1024 * 1024
         ),
     )(image_features, head_weight, text_embeds, natural_exponent_factor, logit_bias)
+    return pl.pallas_call(
+        put_out,
+        out_shape=tuple(jax.ShapeDtypeStruct(a.shape, a.dtype) for a in results),
+        in_specs=[local] * 3,
+        out_specs=[hbm] * 3,
+        scratch_shapes=[dma((3,))],
+        compiler_params=pltpu.CompilerParams(vmem_limit_bytes=8 * 1024 * 1024),
+    )(*results)
 
 
 def solution(mesh):

time: 95.5 us -> 92.5 us (0.969); the launches traced: 93.8 us -> 92.2 us
  local copies, waits for them, and re-layouts: 5.22 us -> 2.91 us
    unnamed x9 -> x6, local copies, waits for them, and re-layouts: 5.22 us -> 2.91 us
    pallas_call x0 -> x1, Pallas kernels: none -> 1.1 us  [on_device(): pl.pallas_call(put_out, out_shape=tuple((jax.ShapeDtypeStruct(a.shape, a....]
where the time goes in v3:
time: 92.5 us; the launch traced here: 92.2 us
  Pallas kernels  87.4 us (94%)
  local copies, waits for them, and re-layouts  2.91 us (3%)
  between operations  1.94 us (2%)
    pallas_call x1, Pallas kernels, on_device(): pl.pallas_call(kernel, out_shape=(jax.ShapeDtypeStruct((R, D), BF16), jax...  86.3 us
    unnamed x6, local copies, waits for them, and re-layouts  2.91 us

profile of v3, /device:TPU:1, one launch (start us, length us, event | category | flops | bytes accessed | tf_op | source)
XLA Modules:
  0.0 92.2 jit_solution(14752488752662769313)
XLA Ops:
  1.9 0.0 copy-start
  1.9 1.1 %copy-done = bf16[256,1536]{1,0:T(8,128)(2,1)S(1)} copy-done((bf16[256,1536]{1,0:T(8,128)(2,1)S(1)}, bf16[256,1536]{1,0:T(8,128)(2,1)}, u32[]{:S(2)}) %copy-start) | copy-done | bytes 786456
  3.1 0.0 copy-start.1
  3.1 1.1 %copy-done.1 = bf16[256,1152]{1,0:T(8,128)(2,1)S(1)} copy-done((bf16[256,1152]{1,0:T(8,128)(2,1)S(1)}, bf16[256,1152]{1,0:T(8,128)(2,1)}, u32[]{:S(2)}) %copy-start.1) | copy-done | bytes 589848
  4.1 0.0 copy-start.2
  4.1 0.7 copy-done.2
  4.8 86.3 %shard_map.76 = (bf16[256,1536]{1,0:T(8,128)(2,1)S(1)}, bf16[256,1152]{1,0:T(8,128)(2,1)S(1)}, f32[6,1152]{1,0:T(8,128)S(1)}) custom-call(bf16[256,1536]{1,0:T(8,128)(2,1)S(1)} %copy-done, bf16[6,1152]{1,0:T(8,128)(2,1)S(1)} %copy-done.2, bf16[256,1152]{1,0:T(8,128)(2,1)S(1)} %copy-done.1, f32[1]{0:T(128)S(6)} %copy.8.nef_ref, f32[1]{0:T(128)S(6)} %copy.9.bias_ref), custom_call_target="tpu_custom_call" | custom-call | tf_op jit(solution)/shard_map/pallas_call | solution.py:531
  91.1 1.1 %shard_map.77 = (bf16[256,1536]{1,0:T(8,128)(2,1)}, bf16[256,1152]{1,0:T(8,128)(2,1)}, f32[6,1152]{1,0:T(8,128)}) custom-call(bf16[256,1536]{1,0:T(8,128)(2,1)S(1)} %get-tuple-element.6.gf, bf16[256,1152]{1,0:T(8,128)(2,1)S(1)} %get-tuple-element.7.gt, f32[6,1152]{1,0:T(8,128)S(1)} %get-tuple-element.8.gw), custom_call_target="tpu_custom_call" | custom-call | tf_op jit(solution)/shard_map/pallas_call | solution.py:575
Async XLA Ops:
  1.9 1.1 %copy-start = (bf16[256,1536]{1,0:T(8,128)(2,1)S(1)}, bf16[256,1536]{1,0:T(8,128)(2,1)}, u32[]{:S(2)}) copy-start(bf16[256,1536]{1,0:T(8,128)(2,1)} %feat_hbm.1) | copy-start | bytes 2359300
  3.1 1.1 %copy-start.1 = (bf16[256,1152]{1,0:T(8,128)(2,1)S(1)}, bf16[256,1152]{1,0:T(8,128)(2,1)}, u32[]{:S(2)}) copy-start(bf16[256,1152]{1,0:T(8,128)(2,1)} %text_hbm.1) | copy-start | bytes 1769476
  4.1 0.7 copy-start.2

commit v4 on v3

--- a/solution.py
+++ b/solution.py
@@ -36,7 +36,7 @@
     feat_hbm, w_hbm, text_hbm, nef_ref, bias_ref,
     gfeat, gtext, gout,
     w_ref, feat, feat2, feat_t, unit, length, img, traw, tlow, tlen, pair, eg,
-    gpart, xbuf, wrow, rbuf, sbuf, xrow, xs, xr, igrad, cross,
+    gpart, xbuf, wrow, rbuf, sbuf, xrow, xs, xr, igrad, cross, cross2,
     in_sem, xw_s, xw_r, ag_s, ag_r, dd_s, dd_r, ex_s, ex_r, rs_s, rs_r, xg_s, xg_r,
 ):
     me = lax.axis_index("blk")
@@ -46,8 +46,20 @@
     y = lax.div(me, ROW * NZ)
     pending = []
 
+    row_y = [lax.rem(y + j, NY) for j in range(NY)]
+    row_z = [lax.rem(z + k, NZ) for k in range(NZ)]
+    dev_y = [v * (NZ * ROW) for v in row_y]
+    dev_z = [v * ROW + r for v in row_z]
+    at_y = [v * YROWS for v in row_y]
+    at_z = [v * BLK for v in row_z]
+
     def dev(dy=0, dz=0):
-        return (lax.rem(y + (dy + NY) , NY) * NZ + lax.rem(z + (dz + NZ), NZ)) * ROW + r
+        return dev_y[dy % NY] + dev_z[dz % NZ]
+
+    wrap = 1 - lax.div(z + (NZ - 1), NZ)
+    first = me - r
+    pre_row = first + wrap * (dev_y[NY - 1] - dev_y[0])
+    below_row = dev(0, -1) - r
 
     def row_dev(k):
         return me - r + lax.rem(r + k, ROW)
@@ -73,8 +85,8 @@
     def arrived(dst, ss, rs):
         remote(dst, dst, ss, rs, near(1)).wait_recv()
 
-    def wblock(ref, yy, zz, c0, cw):
-        start = pl.multiple_of(lax.rem(yy, NY) * YROWS + lax.rem(zz, NZ) * BLK, 8)
+    def wblock(ref, dy, dz, c0, cw):
+        start = pl.multiple_of(at_y[dy % NY] + at_z[dz % NZ], 8)
         return ref.at[pl.ds(start, BLK), pl.ds(c0, cw)]
 
     def transpose(src, col):
@@ -102,7 +114,9 @@
     with jax.named_scope("barrier"):
         barrier = pltpu.get_barrier_semaphore()
         peers = [row_dev(k) for k in range(1, ROW)] + [dev(dz=k) for k in range(1, NZ)]
-        peers += [dev(dy=k) for k in range(1, NY)] + [near(k) for k in (-ROW, -3, -2, -1, 1, 2, 3, ROW)]
+        peers += [dev(d) - r + lax.rem(r + d * -k + ROW, ROW) for d in (-1, 1) for k in (3, 7)]
+        peers += [dev(0, d) - r + lax.rem(r + d * -k + ROW, ROW) for d in (-1, 1) for k in (2, 6)]
+        peers += [dev(dy=k) for k in range(1, NY)] + [near(k) for k in (-ROW, -5, -3, -2, -1, 1, 2, 3, 5, ROW)]
         for peer in peers:
             pl.semaphore_signal(barrier, inc=1, device_id=(peer,), device_id_type=MESH)
         pl.semaphore_wait(barrier, len(peers))
@@ -127,27 +141,6 @@
         send(None, feat, feat2, (ex_s, 12), ex_r.at[0], me + 1 - 2 * core)
         transpose(feat, 0)
 
-    with jax.named_scope("text_send"):
-        @pl.when(core == 0)
-        def _():
-            send(0, tslot(0), tslot(1), (ex_s, 0), ex_r.at[1], near(-1), lambda: tslot(0))
-
-        @pl.when((core == 0) & (r != 0))
-        def _():
-            send("t3", tslot(0), tslot(3), (ex_s, 1), ex_r.at[3], near(-3), lambda: tslot(0))
-
-        @pl.when(core == 1)
-        def _():
-            send(1, tslot(0), tslot(1), (ex_s, 0), ex_r.at[1], near(-1), lambda: tslot(0))
-
-        @pl.when((core == 1) & (r != 1))
-        def _():
-            send("t2", tslot(0), tslot(2), (ex_s, 1), ex_r.at[2], near(-2), lambda: tslot(0))
-
-        @pl.when(r == 1)
-        def _():
-            send("t1", tslot(0), cross, (ex_s, 1), ex_r.at[8], near(6), lambda: tslot(0))
-
     with jax.named_scope("w_row"):
         for k in range(1, ROW):
             arrived(xbuf.at[lax.rem(r + (ROW - k), ROW)], xw_s.at[k], xw_r.at[k])
@@ -156,6 +149,33 @@
         own = pl.multiple_of(y * YROWS + z * BLK, 8)
         w_ref[pl.ds(own, BLK), :] = wrow[...].astype(BF16)
 
+    with jax.named_scope("text_send"):
+        @pl.when((core == 0) & (r != 0))
+        def _():
+            send("t3", tslot(0), tslot(1), (ex_s, 0), ex_r.at[1], near(-1), lambda: tslot(0))
+
+        @pl.when((core == 0) & (r > 2))
+        def _():
+            send("t4", tslot(0), tslot(3), (ex_s, 1), ex_r.at[3], near(-3), lambda: tslot(0))
+
+        @pl.when(core == 1)
+        def _():
+            send(1, tslot(0), tslot(1), (ex_s, 0), ex_r.at[1], near(-1), lambda: tslot(0))
+
+        @pl.when((core == 1) & (r != 1))
+        def _():
+            send("t2", tslot(0), tslot(2), (ex_s, 1), ex_r.at[2], near(-2), lambda: tslot(0))
+
+        @pl.when(r == 0)
+        def _():
+            send("r0", tslot(0), cross, (ex_s, 0), ex_r.at[8], pre_row + 7, lambda: tslot(0))
+            send("r0", tslot(0), cross, (ex_s, 1), ex_r.at[8], pre_row + 3, lambda: tslot(0))
+
+        @pl.when(r == 2)
+        def _():
+            send("r2", tslot(0), cross, (ex_s, 1), ex_r.at[8], pre_row + 5, lambda: tslot(0))
+
+
     def gather(c):
         c0, cw = COLS[c]
         sibling = me + (1 - 2 * c)
@@ -163,17 +183,17 @@
         like = lambda: w_ref.at[pl.ds(0, BLK), pl.ds(c0, cw)]
 
         def put(j, k, dy, dz):
-            part = wblock(w_ref, y + (NY - j), z + (NZ - k), c0, cw)
+            part = wblock(w_ref, -j, -k, c0, cw)
             idx = ((j + dy) % NY) * NZ + (k + dz) % NZ
             send(c, part, part, (ag_s, count[0]), ag_r.at[idx], dev(dy, dz), like)
             count[0] += 1
 
         def share(j, k):
-            part = wblock(w_ref, y + (NY - j), z + (NZ - k), c0, cw)
+            part = wblock(w_ref, -j, -k, c0, cw)
             send(c, part, part, (dd_s, j * NZ + k), dd_r.at[j * NZ + k], sibling, like)
 
         def got(j, k):
-            part = wblock(w_ref, y + (NY - j), z + (NZ - k), c0, cw)
+            part = wblock(w_ref, -j, -k, c0, cw)
             arrived(part, ag_s.at[0], ag_r.at[j * NZ + k])
             return part
 
@@ -217,6 +237,11 @@
         else:
             for j in (1, 3, 2):
                 put(0, 0, j, 0)
+
+            @pl.when((r == 1) & (z == 0))
+            def _():
+                send("r1z", tslot(0), cross, (ex_s, 1), ex_r.at[8], pre_row + 1, lambda: tslot(0))
+
             for j in (0, 1, 3, 2):
                 if j:
                     got(j, 0)
@@ -229,38 +254,53 @@
             for h in (1, 2, 3):
                 for j in (0, 1, 3, 2):
                     got(j, h)
-                    if h < 3 or j in (0, 3):
-                        put(j, h, 0, 1)
+                    put(j, h, 0, 1)
                     share(j, h)
                     got(j, NZ - h)
-                    if h < 3 or j in (1, 2):
+                    if h < 3:
                         put(j, NZ - h, 0, -1)
                     share(j, NZ - h)
-                if h == 2:
-
-                    @pl.when(r == ROW - 1)
+                if h == 3:
+
+                    @pl.when((r > 1) | (z == 0))
                     def _():
                         arrived(cross, ex_s.at[0], ex_r.at[8])
-                        send("t7", cross, tslot(2), (ex_s, 2), ex_r.at[2], near(-ROW), lambda: tslot(0))
-
-                if h == 3:
-                    arrived(tslot(1), ex_s.at[0], ex_r.at[1])
-                    send(1, tslot(1), tslot(2), (ex_s, 3), ex_r.at[2], near(-1), lambda: tslot(0))
-
-                    @pl.when(r == ROW - 1)
+
+                    @pl.when((r == 1) & (z == 0))
                     def _():
-                        send("t7", tslot(1), tslot(3), (ex_s, 4), ex_r.at[3], near(-2), lambda: tslot(0))
+                        send("r1z", cross, tslot(2), (ex_s, 2), ex_r.at[2], below_row + 7, lambda: tslot(0))
+
+                    @pl.when((r == 1) & (z != 0))
+                    def _():
+                        send("r1n", tslot(0), tslot(2), (ex_s, 1), ex_r.at[2], below_row + 7, lambda: tslot(0))
+
+                    @pl.when(r == 3)
+                    def _():
+                        send("r3", cross, tslot(3), (ex_s, 2), ex_r.at[3], below_row + 5, lambda: tslot(0))
+
+                    @pl.when(r == 5)
+                    def _():
+                        send("r5", cross, tslot(3), (ex_s, 2), ex_r.at[3], below_row + 7, lambda: tslot(0))
+
+                    @pl.when(r == 7)
+                    def _():
+                        send("r7", cross, tslot(1), (ex_s, 2), ex_r.at[1], below_row + 7, lambda: tslot(0))
 
             for j in (0, 1, 3, 2):
                 got(j, 4)
                 share(j, 4)
-            arrived(tslot(2), ex_s.at[0], ex_r.at[2])
-            send(1, tslot(2), tslot(3), (ex_s, 10), ex_r.at[3], near(-1), lambda: tslot(0))
+            @pl.when(r != ROW - 1)
+            def _():
+                arrived(tslot(1), ex_s.at[0], ex_r.at[1])
+                send("o7", tslot(1), tslot(2), (ex_s, 3), ex_r.at[2], near(-1), lambda: tslot(0))
+                arrived(tslot(2), ex_s.at[0], ex_r.at[2])
+                send("o7", tslot(2), tslot(3), (ex_s, 10), ex_r.at[3], near(-1), lambda: tslot(0))
+
         o0, ow = COLS[1 - c]
         for j in range(NY):
             for k in range(NZ):
                 if j or k:
-                    part = wblock(w_ref, y + (NY - j), z + (NZ - k), o0, ow)
+                    part = wblock(w_ref, -j, -k, o0, ow)
                     arrived(part, dd_s.at[0], dd_r.at[j * NZ + k])
 
     with jax.named_scope("gather"):
@@ -286,12 +326,31 @@
             length[rows, :] = inv
             img[rows, :] = u.astype(BF16)
 
+    @pl.when(r == ROW - 1)
+    def _():
+        arrived(tslot(1), ex_s.at[0], ex_r.at[1])
+        send("r7", tslot(1), tslot(2), (ex_s, 3), ex_r.at[2], near(-1), lambda: tslot(0))
+        arrived(tslot(2), ex_s.at[0], ex_r.at[2])
+        send("r7", tslot(2), tslot(3), (ex_s, 10), ex_r.at[3], near(-1), lambda: tslot(0))
+
     with jax.named_scope("image_send"):
+        i3 = (core == 1) & (r != ROW - 1) & (r != 5)
+
+        @pl.when(r == 5)
+        def _():
+            send("i5", slot(0), cross2, (ex_s, 6), ex_r.at[9], near(5), lambda: slot(0))
+
+        @pl.when(r == ROW - 2)
+        def _():
+            send("i6", slot(0), cross2, (ex_s, 6), ex_r.at[9], first, lambda: slot(0))
+
+        i5_early = (core == 1) & (r != ROW - 1) & ((r != 5) | (z != NZ - 1))
+
         @pl.when(core == 1)
         def _():
             send(1, slot(0), slot(1), (ex_s, 5), ex_r.at[5], near(1), lambda: slot(0))
 
-        @pl.when((core == 1) & (r != ROW - 1))
+        @pl.when(i3)
         def _():
             send("i3", slot(0), slot(3), (ex_s, 6), ex_r.at[7], near(3), lambda: slot(0))
 
@@ -302,10 +361,6 @@
         @pl.when((core == 0) & (r != ROW - 2))
         def _():
             send("i2", slot(0), slot(2), (ex_s, 6), ex_r.at[6], near(2), lambda: slot(0))
-
-        @pl.when(r == ROW - 2)
-        def _():
-            send("i6", slot(0), cross, (ex_s, 6), ex_r.at[9], near(-6), lambda: slot(0))
 
     factor = jnp.exp(jnp.full((1, R), nef_ref[0], F32))
     bias = bias_ref[0]
@@ -368,11 +423,11 @@
         arrived(eg.at[pl.ds(R, R), pl.ds(c0, cw)], ex_s.at[0], ex_r.at[10])
 
         def product(j):
-            rows = pl.ds(pl.multiple_of(lax.rem(y + j, NY) * YROWS, 8), YROWS)
+            rows = pl.ds(pl.multiple_of(at_y[j], 8), YROWS)
             gpart[rows, pl.ds(0, cw)] = dot(feat_t[rows, :], eg[:, pl.ds(c0, cw)]).astype(BF16)
 
         def mine(dy, dz):
-            return wblock(gpart, y + (dy + NY), z + (dz + NZ), 0, cw)
+            return wblock(gpart, dy, dz, 0, cw)
 
         def buf(i):
             return rbuf.at[i, :, pl.ds(0, cw)]
@@ -399,37 +454,45 @@
                 emit(other, 8 + k if step == -1 else 16 + k, -step, 0)
                 part[...] = (part[...].astype(F32) + take(k)).astype(BF16)
                 emit(part, 8 + k if step == 1 else 16 + k, step, 0)
-            arrived(slot(1), ex_s.at[0], ex_r.at[5])
-            send(0, slot(1), slot(2), (ex_s, 8), ex_r.at[6], near(1), lambda: slot(0))
+            @pl.when((r == 0) | (r == 2))
+            def _():
+                arrived(cross2, ex_s.at[0], ex_r.at[9])
 
             @pl.when(r == 0)
             def _():
-                send("i0", slot(1), slot(3), (ex_s, 7), ex_r.at[7], near(2), lambda: slot(0))
-                arrived(cross, ex_s.at[0], ex_r.at[9])
-                send("i0", cross, slot(2), (ex_s, 13), ex_r.at[6], near(ROW), lambda: slot(0))
+                send("i0", cross2, slot(2), (ex_s, 13), ex_r.at[6], near(ROW), lambda: slot(0))
+
+            @pl.when(r == 2)
+            def _():
+                send("i2r", cross2, slot(3), (ex_s, 13), ex_r.at[7], first, lambda: slot(0))
 
             for i, k in enumerate(Z_ORDER + (0,)):
                 total = mine(0, k)[...].astype(F32) + take(8 + k) + take(16 + k)
                 if k:
                     sbuf[k, :, pl.ds(0, cw)] = total.astype(BF16)
                     emit(sbuf.at[k, :, pl.ds(0, cw)], 24 + k, 0, k)
-            arrived(slot(2), ex_s.at[0], ex_r.at[6])
-            send(0, slot(2), slot(3), (ex_s, 11), ex_r.at[7], near(1), lambda: slot(0))
+            arrived(slot(1), ex_s.at[0], ex_r.at[5])
+            send(0, slot(1), slot(2), (ex_s, 8), ex_r.at[6], near(1), lambda: slot(0))
+
+            @pl.when(r == 0)
+            def _():
+                send("i0", slot(1), slot(3), (ex_s, 7), ex_r.at[7], near(2), lambda: slot(0))
+
+
             for k in Z_ARRIVAL[1:]:
                 total = total + take(24 + k)
         else:
             for j in range(NY):
                 product(j)
             order = (2, 1, 3, 0)
-            plus, minus = (2, 1), (3, 0)
             for j in order:
-                emit(mine(j, 4), j if j in plus else 16 + j, 0, 1 if j in plus else -1)
+                emit(mine(j, 4), 16 + j, 0, -1)
             for h in (3, 2, 1):
                 s = 3 - h
                 for j in order:
                     for sign, base in ((1, 0), (-1, 16)):
                         part = mine(j, sign * h)
-                        if s or j in (plus if sign == 1 else minus):
+                        if s or sign == -1:
                             part[...] = (part[...].astype(F32) + take(base + 4 * s + j)).astype(BF16)
                         emit(part, base + 4 * (s + 1) + j, 0, sign)
             for j in order:
@@ -460,12 +523,18 @@
             reduce_weight(1)
 
     with jax.named_scope("image_wait"):
+        @pl.when(core == 0)
+        def _():
+            arrived(slot(2), ex_s.at[0], ex_r.at[6])
+            send(0, slot(2), slot(3), (ex_s, 11), ex_r.at[7], near(1), lambda: slot(0))
+
         @pl.when(core == 1)
         def _():
             arrived(slot(1), ex_s.at[0], ex_r.at[5])
             arrived(slot(2), ex_s.at[0], ex_r.at[6])
 
         arrived(slot(3), ex_s.at[0], ex_r.at[7])
+
     with jax.named_scope("text_side"):
         for s in range(S):
             pair[:, pl.ds(s * R, R)] = derivative(dot_nt(tlow[pl.ds(0, R), :], img[pl.ds(s * R, R), :]), s == 0)
@@ -502,9 +571,10 @@
             if only is None:
                 wait()
         groups = {
-            0: core == 0, 1: core == 1, "t1": r == 1, "t7": r == ROW - 1, "i6": r == ROW - 2, "i0": r == 0,
-            "t3": (core == 0) & (r != 0), "t2": (core == 1) & (r != 1),
-            "i3": (core == 1) & (r != ROW - 1), "i2": (core == 0) & (r != ROW - 2),
+            0: core == 0, 1: core == 1, "r0": r == 0, "r2": r == 2, "r3": r == 3, "r5": r == 5, "r1z": (r == 1) & (z == 0), "r1n": (r == 1) & (z != 0), "r7": r == ROW - 1, "i0": r == 0,
+            "o7": (core == 1) & (r != ROW - 1), "t3": (core == 0) & (r != 0), "t4": (core == 0) & (r > 2),
+            "t2": (core == 1) & (r != 1), "i3": i3, "i5": r == 5, "i2r": r == 2, "i6": r == ROW - 2,
+            "i2": (core == 0) & (r != ROW - 2),
         }
         for group, inside in groups.items():
 
@@ -560,6 +630,7 @@
             pltpu.VMEM((ROW, SH, W1), F32),
             pltpu.VMEM((R, E), F32),
             pltpu.VMEM((R, E), BF16),
+            pltpu.VMEM((R, E), BF16),
             dma((3,)),
             dma((ROW,)), dma((ROW,)),
             dma((32,)), dma((32,)),

time: 92.5 us -> 85.6 us (0.925)
  the two profiles are of different devices: /device:TPU:1 before, /device:TPU:10 now
where the time goes in v4:
time: 85.6 us; the launch traced here: 85.4 us
  Pallas kernels  80.5 us (94%)
  local copies, waits for them, and re-layouts  2.91 us (3%)
  between operations  1.94 us (2%)
    pallas_call x1, Pallas kernels, on_device(): pl.pallas_call(kernel, out_shape=(jax.ShapeDtypeStruct((R, D), BF16), jax...  79.4 us
    unnamed x6, local copies, waits for them, and re-layouts  2.91 us

profile of v4, /device:TPU:10, one launch (start us, length us, event | category | flops | bytes accessed | tf_op | source)
XLA Modules:
  0.0 85.4 jit_solution(6727036959778046716)
XLA Ops:
  1.9 0.0 copy-start
  1.9 1.1 %copy-done = bf16[256,1536]{1,0:T(8,128)(2,1)S(1)} copy-done((bf16[256,1536]{1,0:T(8,128)(2,1)S(1)}, bf16[256,1536]{1,0:T(8,128)(2,1)}, u32[]{:S(2)}) %copy-start) | copy-done | bytes 786456
  3.1 0.0 copy-start.1
  3.1 1.1 %copy-done.1 = bf16[256,1152]{1,0:T(8,128)(2,1)S(1)} copy-done((bf16[256,1152]{1,0:T(8,128)(2,1)S(1)}, bf16[256,1152]{1,0:T(8,128)(2,1)}, u32[]{:S(2)}) %copy-start.1) | copy-done | bytes 589848
  4.1 0.0 copy-start.2
  4.1 0.7 copy-done.2
  4.8 79.4 %shard_map.76 = (bf16[256,1536]{1,0:T(8,128)(2,1)S(1)}, bf16[256,1152]{1,0:T(8,128)(2,1)S(1)}, f32[6,1152]{1,0:T(8,128)S(1)}) custom-call(bf16[256,1536]{1,0:T(8,128)(2,1)S(1)} %copy-done, bf16[6,1152]{1,0:T(8,128)(2,1)S(1)} %copy-done.2, bf16[256,1152]{1,0:T(8,128)(2,1)S(1)} %copy-done.1, f32[1]{0:T(128)S(6)} %copy.8.nef_ref, f32[1]{0:T(128)S(6)} %copy.9.bias_ref), custom_call_target="tpu_custom_call" | custom-call | tf_op jit(solution)/shard_map/pallas_call | solution.py:601
  84.3 1.1 %shard_map.77 = (bf16[256,1536]{1,0:T(8,128)(2,1)}, bf16[256,1152]{1,0:T(8,128)(2,1)}, f32[6,1152]{1,0:T(8,128)}) custom-call(bf16[256,1536]{1,0:T(8,128)(2,1)S(1)} %get-tuple-element.6.gf, bf16[256,1152]{1,0:T(8,128)(2,1)S(1)} %get-tuple-element.7.gt, f32[6,1152]{1,0:T(8,128)S(1)} %get-tuple-element.8.gw), custom_call_target="tpu_custom_call" | custom-call | tf_op jit(solution)/shard_map/pallas_call | solution.py:646
Async XLA Ops:
  1.9 1.1 %copy-start = (bf16[256,1536]{1,0:T(8,128)(2,1)S(1)}, bf16[256,1536]{1,0:T(8,128)(2,1)}, u32[]{:S(2)}) copy-start(bf16[256,1536]{1,0:T(8,128)(2,1)} %feat_hbm.1) | copy-start | bytes 2359300
  3.1 1.1 %copy-start.1 = (bf16[256,1152]{1,0:T(8,128)(2,1)S(1)}, bf16[256,1152]{1,0:T(8,128)(2,1)}, u32[]{:S(2)}) copy-start(bf16[256,1152]{1,0:T(8,128)(2,1)} %text_hbm.1) | copy-start | bytes 1769476
  4.1 0.7 copy-start.2

commit v5 on v4

--- a/solution.py
+++ b/solution.py
@@ -15,6 +15,7 @@
 YROWS = BLK * NZ
 W1 = 640
 COLS = ((0, W1), (W1, E - W1))
+FAR, NEAR = 5, 0
 Y_CORE = 0
 EPS = 1e-06
 TILES = ((0, 512), (512, 512), (1024, 128))
@@ -114,7 +115,7 @@
     with jax.named_scope("barrier"):
         barrier = pltpu.get_barrier_semaphore()
         peers = [row_dev(k) for k in range(1, ROW)] + [dev(dz=k) for k in range(1, NZ)]
-        peers += [dev(d) - r + lax.rem(r + d * -k + ROW, ROW) for d in (-1, 1) for k in (3, 7)]
+        peers += [dev(d) - r + lax.rem(r + d * -k + ROW, ROW) for d in (-1, 1) for k in (1, 3, 7)]
         peers += [dev(0, d) - r + lax.rem(r + d * -k + ROW, ROW) for d in (-1, 1) for k in (2, 6)]
         peers += [dev(dy=k) for k in range(1, NY)] + [near(k) for k in (-ROW, -5, -3, -2, -1, 1, 2, 3, 5, ROW)]
         for peer in peers:
@@ -208,17 +209,19 @@
                     got(0, k)
                 put(0, k, 1, 0)
                 put(0, k, -1, 0)
+                if i >= FAR:
+                    put(0, k, 2, 0)
                 if k:
                     share(0, k)
 
             def stage2(i):
                 k = Z_ARRIVAL[i]
                 got(1, k)
-                if i % 2 == 0:
+                if i < FAR and i % 2 == 0:
                     put(1, k, 1, 0)
                 share(1, k)
                 got(3, k)
-                if i % 2 == 1:
+                if i < FAR and i % 2 == 1:
                     put(3, k, -1, 0)
                 share(3, k)
 
@@ -335,20 +338,25 @@
 
     with jax.named_scope("image_send"):
         i3 = (core == 1) & (r != ROW - 1) & (r != 5)
+        last = z == NZ - 1
+        i7_last = (r == ROW - 1) & last
+
+        @pl.when(i7_last)
+        def _():
+            send("i7", slot(0), cross2, (ex_s, 5), ex_r.at[9], dev(1) - 1, lambda: slot(0))
+            send("i7", slot(0), cross2, (ex_s, 6), ex_r.at[9], dev(1) - 3, lambda: slot(0))
+
+        early = (r == 0) & (z != 0)
 
         @pl.when(r == 5)
         def _():
             send("i5", slot(0), cross2, (ex_s, 6), ex_r.at[9], near(5), lambda: slot(0))
 
-        @pl.when(r == ROW - 2)
-        def _():
-            send("i6", slot(0), cross2, (ex_s, 6), ex_r.at[9], first, lambda: slot(0))
-
         i5_early = (core == 1) & (r != ROW - 1) & ((r != 5) | (z != NZ - 1))
 
-        @pl.when(core == 1)
-        def _():
-            send(1, slot(0), slot(1), (ex_s, 5), ex_r.at[5], near(1), lambda: slot(0))
+        @pl.when((core == 1) & ((r != ROW - 1) | (z != NZ - 1)))
+        def _():
+            send("i1", slot(0), slot(1), (ex_s, 5), ex_r.at[5], near(1), lambda: slot(0))
 
         @pl.when(i3)
         def _():
@@ -410,12 +418,13 @@
             part = pl.ds(COLS[0][0], COLS[0][1])
             send(1, eg.at[pl.ds(0, R), part], eg.at[pl.ds(R, R), part], (ex_s, 9), ex_r.at[10], me - 1, lambda: eg.at[pl.ds(0, R), pl.ds(COLS[0][0], COLS[0][1])])
 
+    def feature_gradient(i):
+        cols = pl.ds(i * 512, 512)
+        gfeat[:, cols] = dot_nt(eg[pl.ds(0, R), :], w_ref[cols, :]).astype(BF16)
+
     with jax.named_scope("feat_grad"):
-        @pl.loop(0, D // 512)
-        def _(i):
-            cols = pl.ds(pl.multiple_of(i * 512, 512), 512)
-            gfeat[:, cols] = dot_nt(eg[pl.ds(0, R), :], w_ref[cols, :]).astype(BF16)
-
+        feature_gradient(0)
+        feature_gradient(1)
 
     def reduce_weight(c):
         c0, cw = COLS[c]
@@ -442,42 +451,58 @@
 
         if c == Y_CORE:
             product(2)
+
+            @pl.when(r == ROW - 2)
+            def _():
+                send("i6", slot(0), cross2, (ex_s, 6), ex_r.at[9], first, lambda: slot(0))
+
             for i, k in enumerate(Z_ORDER + (0,)):
-                emit(mine(2, k), k, 1 if i % 2 == 0 else -1, 0)
+                emit(mine(2, k), k, 2 if i < NEAR else 1 if i % 2 == 0 else -1, 0)
             product(1)
             product(3)
             product(0)
+            feature_gradient(2)
             for i, k in enumerate(Z_ORDER + (0,)):
                 step = 1 if i % 2 == 0 else -1
                 part = mine(step, k)
                 other = mine(-step, k)
                 emit(other, 8 + k if step == -1 else 16 + k, -step, 0)
-                part[...] = (part[...].astype(F32) + take(k)).astype(BF16)
+                if i >= NEAR:
+                    part[...] = (part[...].astype(F32) + take(k)).astype(BF16)
                 emit(part, 8 + k if step == 1 else 16 + k, step, 0)
-            @pl.when((r == 0) | (r == 2))
+            @pl.when(r == 2)
             def _():
                 arrived(cross2, ex_s.at[0], ex_r.at[9])
-
-            @pl.when(r == 0)
-            def _():
-                send("i0", cross2, slot(2), (ex_s, 13), ex_r.at[6], near(ROW), lambda: slot(0))
-
-            @pl.when(r == 2)
-            def _():
                 send("i2r", cross2, slot(3), (ex_s, 13), ex_r.at[7], first, lambda: slot(0))
 
             for i, k in enumerate(Z_ORDER + (0,)):
                 total = mine(0, k)[...].astype(F32) + take(8 + k) + take(16 + k)
+                if i < NEAR:
+                    total = total + take(k)
                 if k:
                     sbuf[k, :, pl.ds(0, cw)] = total.astype(BF16)
                     emit(sbuf.at[k, :, pl.ds(0, cw)], 24 + k, 0, k)
-            arrived(slot(1), ex_s.at[0], ex_r.at[5])
-            send(0, slot(1), slot(2), (ex_s, 8), ex_r.at[6], near(1), lambda: slot(0))
-
             @pl.when(r == 0)
             def _():
-                send("i0", slot(1), slot(3), (ex_s, 7), ex_r.at[7], near(2), lambda: slot(0))
-
+                arrived(cross2, ex_s.at[0], ex_r.at[9])
+                send("i0", cross2, slot(2), (ex_s, 13), ex_r.at[6], near(ROW), lambda: slot(0))
+
+            @pl.when(((r == 4) | (r == 6)) & last)
+            def _():
+                arrived(cross2, ex_s.at[0], ex_r.at[9])
+
+            @pl.when((r == 6) & last)
+            def _():
+                send("i6r", cross2, slot(1), (ex_s, 13), ex_r.at[5], dev(0, 1) - r, lambda: slot(0))
+
+            @pl.when((r == 4) & last)
+            def _():
+                send("i4r", cross2, slot(3), (ex_s, 13), ex_r.at[7], dev(0, 1) - r + 2, lambda: slot(0))
+
+            @pl.when(early)
+            def _():
+                arrived(slot(1), ex_s.at[0], ex_r.at[5])
+                send("i0e", slot(1), slot(3), (ex_s, 7), ex_r.at[7], near(2), lambda: slot(0))
 
             for k in Z_ARRIVAL[1:]:
                 total = total + take(24 + k)
@@ -487,6 +512,7 @@
             order = (2, 1, 3, 0)
             for j in order:
                 emit(mine(j, 4), 16 + j, 0, -1)
+            feature_gradient(2)
             for h in (3, 2, 1):
                 s = 3 - h
                 for j in order:
@@ -523,8 +549,13 @@
             reduce_weight(1)
 
     with jax.named_scope("image_wait"):
+        @pl.when((core == 0) & ((r != 0) | (z == 0)))
+        def _():
+            arrived(slot(1), ex_s.at[0], ex_r.at[5])
+
         @pl.when(core == 0)
         def _():
+            send(0, slot(1), slot(2), (ex_s, 8), ex_r.at[6], near(1), lambda: slot(0))
             arrived(slot(2), ex_s.at[0], ex_r.at[6])
             send(0, slot(2), slot(3), (ex_s, 11), ex_r.at[7], near(1), lambda: slot(0))
 
@@ -573,7 +604,8 @@
         groups = {
             0: core == 0, 1: core == 1, "r0": r == 0, "r2": r == 2, "r3": r == 3, "r5": r == 5, "r1z": (r == 1) & (z == 0), "r1n": (r == 1) & (z != 0), "r7": r == ROW - 1, "i0": r == 0,
             "o7": (core == 1) & (r != ROW - 1), "t3": (core == 0) & (r != 0), "t4": (core == 0) & (r > 2),
-            "t2": (core == 1) & (r != 1), "i3": i3, "i5": r == 5, "i2r": r == 2, "i6": r == ROW - 2,
+            "t2": (core == 1) & (r != 1), "i3": i3, "i0e": early, "i7": i7_last, "i6r": (r == 6) & last, "i4r": (r == 4) & last, "i1": (core == 1) & ((r != ROW - 1) | (z != NZ - 1)),
+            "i5": r == 5, "i2r": r == 2, "i6": r == ROW - 2,
             "i2": (core == 0) & (r != ROW - 2),
         }
         for group, inside in groups.items():
@@ -640,7 +672,7 @@
             dma((ROW,)), dma((ROW,)),
         ],
         compiler_params=pltpu.CompilerParams(
-            collective_id=0, has_side_effects=True, vmem_limit_bytes=32 * 1024 * 1024
+            collective_id=0, has_side_effects=True, vmem_limit_bytes=52 * 1024 * 1024
         ),
     )(image_features, head_weight, text_embeds, natural_exponent_factor, logit_bias)
     return pl.pallas_call(

time: 85.6 us -> 85.6 us (level)
  the two profiles are of different devices: /device:TPU:10 before, /device:TPU:1 now
where the time goes in v5:
time: 85.6 us; the launch traced here: 85.4 us
  Pallas kernels  81.7 us (95%)
  between operations  1.94 us (2%)
  local copies, waits for them, and re-layouts  1.78 us (2%)
    pallas_call x1, Pallas kernels, on_device(): pl.pallas_call(kernel, out_shape=(jax.ShapeDtypeStruct((R, D), BF16), jax...  80.6 us
    unnamed x4, local copies, waits for them, and re-layouts  1.78 us

profile of v5, /device:TPU:1, one launch (start us, length us, event | category | flops | bytes accessed | tf_op | source)
XLA Modules:
  0.0 85.4 jit_solution(18298355037065445001)
XLA Ops:
  1.9 0.0 copy-start
  1.9 1.1 %copy-done = bf16[256,1152]{1,0:T(8,128)(2,1)S(1)} copy-done((bf16[256,1152]{1,0:T(8,128)(2,1)S(1)}, bf16[256,1152]{1,0:T(8,128)(2,1)}, u32[]{:S(2)}) %copy-start) | copy-done | bytes 589848
  3.0 0.0 copy-start.1
  3.0 0.7 copy-done.1
  3.7 80.6 %shard_map.76 = (bf16[256,1536]{1,0:T(8,128)(2,1)S(1)}, bf16[256,1152]{1,0:T(8,128)(2,1)S(1)}, f32[6,1152]{1,0:T(8,128)S(1)}) custom-call(bf16[256,1536]{1,0:T(8,128)(2,1)} %feat_hbm.1, bf16[6,1152]{1,0:T(8,128)(2,1)S(1)} %copy-done.1, bf16[256,1152]{1,0:T(8,128)(2,1)S(1)} %copy-done, f32[1]{0:T(128)S(6)} %copy.8.nef_ref, f32[1]{0:T(128)S(6)} %copy.9.bias_ref), custom_call_target="tpu_custom_call" | custom-call | tf_op jit(solution)/shard_map/pallas_call | solution.py:633
  84.3 1.1 %shard_map.77 = (bf16[256,1536]{1,0:T(8,128)(2,1)}, bf16[256,1152]{1,0:T(8,128)(2,1)}, f32[6,1152]{1,0:T(8,128)}) custom-call(bf16[256,1536]{1,0:T(8,128)(2,1)S(1)} %get-tuple-element.6.gf, bf16[256,1152]{1,0:T(8,128)(2,1)S(1)} %get-tuple-element.7.gt, f32[6,1152]{1,0:T(8,128)S(1)} %get-tuple-element.8.gw), custom_call_target="tpu_custom_call" | custom-call | tf_op jit(solution)/shard_map/pallas_call | solution.py:678
Async XLA Ops:
  1.9 1.1 %copy-start = (bf16[256,1152]{1,0:T(8,128)(2,1)S(1)}, bf16[256,1152]{1,0:T(8,128)(2,1)}, u32[]{:S(2)}) copy-start(bf16[256,1152]{1,0:T(8,128)(2,1)} %text_hbm.1) | copy-start | bytes 1769476
  3.0 0.7 copy-start.1

commit v6 on v5

--- a/solution.py
+++ b/solution.py
@@ -16,6 +16,8 @@
 W1 = 640
 COLS = ((0, W1), (W1, E - W1))
 FAR, NEAR = 5, 0
+W2 = 768
+RCOLS = ((0, W2), (W2, E - W2))
 Y_CORE = 0
 EPS = 1e-06
 TILES = ((0, 512), (512, 512), (1024, 128))
@@ -130,7 +132,7 @@
     with jax.named_scope("own_text"):
         cp_t.wait()
 
-        @pl.loop(0, R // 32)
+        @pl.loop(0, R // 32, unroll=2)
         def _(i):
             rows = pl.ds(pl.multiple_of(i * 32, 32), 32)
             t = traw[rows, :].astype(F32)
@@ -319,7 +321,7 @@
         for c0, cw in TILES:
             unit[:, pl.ds(c0, cw)] = dot(feat[...], w_ref[:, pl.ds(c0, cw)])
 
-        @pl.loop(0, R // 32)
+        @pl.loop(0, R // 32, unroll=2)
         def _(i):
             rows = pl.ds(pl.multiple_of(i * 32, 32), 32)
             e = unit[rows, :]
@@ -402,7 +404,7 @@
         for c0, cw in TILES:
             igrad[:, pl.ds(c0, cw)] = dot(pair[...], tlow[:, pl.ds(c0, cw)])
 
-        @pl.loop(0, R // 32)
+        @pl.loop(0, R // 32, unroll=2)
         def _(i):
             rows = pl.ds(pl.multiple_of(i * 32, 32), 32)
             eg[rows, :] = back(igrad[rows, :], unit[rows, :], length[rows, :]).astype(BF16)
@@ -410,13 +412,13 @@
     with jax.named_scope("eg_send"):
         @pl.when(core == 0)
         def _():
-            part = pl.ds(COLS[1][0], COLS[1][1])
-            send(0, eg.at[pl.ds(0, R), part], eg.at[pl.ds(R, R), part], (ex_s, 9), ex_r.at[10], me + 1, lambda: eg.at[pl.ds(0, R), pl.ds(COLS[1][0], COLS[1][1])])
+            part = pl.ds(RCOLS[1][0], RCOLS[1][1])
+            send(0, eg.at[pl.ds(0, R), part], eg.at[pl.ds(R, R), part], (ex_s, 9), ex_r.at[10], me + 1, lambda: eg.at[pl.ds(0, R), pl.ds(RCOLS[1][0], RCOLS[1][1])])
 
         @pl.when(core == 1)
         def _():
-            part = pl.ds(COLS[0][0], COLS[0][1])
-            send(1, eg.at[pl.ds(0, R), part], eg.at[pl.ds(R, R), part], (ex_s, 9), ex_r.at[10], me - 1, lambda: eg.at[pl.ds(0, R), pl.ds(COLS[0][0], COLS[0][1])])
+            part = pl.ds(RCOLS[0][0], RCOLS[0][1])
+            send(1, eg.at[pl.ds(0, R), part], eg.at[pl.ds(R, R), part], (ex_s, 9), ex_r.at[10], me - 1, lambda: eg.at[pl.ds(0, R), pl.ds(RCOLS[0][0], RCOLS[0][1])])
 
     def feature_gradient(i):
         cols = pl.ds(i * 512, 512)
@@ -427,7 +429,7 @@
         feature_gradient(1)
 
     def reduce_weight(c):
-        c0, cw = COLS[c]
+        c0, cw = RCOLS[c]
         count = [0]
         arrived(eg.at[pl.ds(R, R), pl.ds(c0, cw)], ex_s.at[0], ex_r.at[10])
 
@@ -548,6 +550,9 @@
         def _():
             reduce_weight(1)
 
+    def similarities(s):
+        pair[:, pl.ds(s * R, R)] = derivative(dot_nt(tlow[pl.ds(0, R), :], img[pl.ds(s * R, R), :]), s == 0)
+
     with jax.named_scope("image_wait"):
         @pl.when((core == 0) & ((r != 0) | (z == 0)))
         def _():
@@ -556,23 +561,39 @@
         @pl.when(core == 0)
         def _():
             send(0, slot(1), slot(2), (ex_s, 8), ex_r.at[6], near(1), lambda: slot(0))
+
+        @pl.when((core == 0) & (r != 0))
+        def _():
             arrived(slot(2), ex_s.at[0], ex_r.at[6])
-            send(0, slot(2), slot(3), (ex_s, 11), ex_r.at[7], near(1), lambda: slot(0))
+            send("s2", slot(2), slot(3), (ex_s, 11), ex_r.at[7], near(1), lambda: slot(0))
 
         @pl.when(core == 1)
         def _():
             arrived(slot(1), ex_s.at[0], ex_r.at[5])
+
+        for s in range(2):
+            similarities(s)
+        for c0, cw in TILES:
+            igrad[:, pl.ds(c0, cw)] = dot(pair[:, pl.ds(0, 2 * R)], img[pl.ds(0, 2 * R), pl.ds(c0, cw)])
+
+        @pl.when(r == 0)
+        def _():
             arrived(slot(2), ex_s.at[0], ex_r.at[6])
-
+            send("s0", slot(2), slot(3), (ex_s, 11), ex_r.at[7], near(1), lambda: slot(0))
+
+        @pl.when(core == 1)
+        def _():
+            arrived(slot(2), ex_s.at[0], ex_r.at[6])
+
+        similarities(2)
         arrived(slot(3), ex_s.at[0], ex_r.at[7])
 
     with jax.named_scope("text_side"):
-        for s in range(S):
-            pair[:, pl.ds(s * R, R)] = derivative(dot_nt(tlow[pl.ds(0, R), :], img[pl.ds(s * R, R), :]), s == 0)
+        similarities(3)
         for c0, cw in TILES:
-            igrad[:, pl.ds(c0, cw)] = dot(pair[...], img[:, pl.ds(c0, cw)])
-
-        @pl.loop(0, R // 32)
+            igrad[:, pl.ds(c0, cw)] += dot(pair[:, pl.ds(2 * R, 2 * R)], img[pl.ds(2 * R, 2 * R), pl.ds(c0, cw)])
+
+        @pl.loop(0, R // 32, unroll=2)
         def _(i):
             rows = pl.ds(pl.multiple_of(i * 32, 32), 32)
             inv = tlen[rows, :]
@@ -584,14 +605,14 @@
 
             @pl.when(lax.rem(source, 2) == 1)
             def _():
-                arrived(xr.at[source, :, pl.ds(0, COLS[1][1])], xg_s.at[k], xg_r.at[k])
+                arrived(xr.at[source, :, pl.ds(0, RCOLS[1][1])], xg_s.at[k], xg_r.at[k])
 
             @pl.when(lax.rem(source, 2) == 0)
             def _():
-                arrived(xr.at[source, :, pl.ds(0, COLS[0][1])], xg_s.at[k], xg_r.at[k])
+                arrived(xr.at[source, :, pl.ds(0, RCOLS[0][1])], xg_s.at[k], xg_r.at[k])
 
         for c in range(2):
-            c0, cw = COLS[c]
+            c0, cw = RCOLS[c]
             total = xr[c, :, pl.ds(0, cw)]
             for k in range(1, NX):
                 total = total + xr[2 * k + c, :, pl.ds(0, cw)]
@@ -604,7 +625,7 @@
         groups = {
             0: core == 0, 1: core == 1, "r0": r == 0, "r2": r == 2, "r3": r == 3, "r5": r == 5, "r1z": (r == 1) & (z == 0), "r1n": (r == 1) & (z != 0), "r7": r == ROW - 1, "i0": r == 0,
             "o7": (core == 1) & (r != ROW - 1), "t3": (core == 0) & (r != 0), "t4": (core == 0) & (r > 2),
-            "t2": (core == 1) & (r != 1), "i3": i3, "i0e": early, "i7": i7_last, "i6r": (r == 6) & last, "i4r": (r == 4) & last, "i1": (core == 1) & ((r != ROW - 1) | (z != NZ - 1)),
+            "t2": (core == 1) & (r != 1), "i3": i3, "s0": r == 0, "s2": (core == 0) & (r != 0), "i0e": early, "i7": i7_last, "i6r": (r == 6) & last, "i4r": (r == 4) & last, "i1": (core == 1) & ((r != ROW - 1) | (z != NZ - 1)),
             "i5": r == 5, "i2r": r == 2, "i6": r == ROW - 2,
             "i2": (core == 0) & (r != ROW - 2),
         }
@@ -652,14 +673,14 @@
             pltpu.VMEM((R, 1), F32),
             pltpu.VMEM((R, S * R), BF16),
             pltpu.VMEM((2 * R, E), BF16),
-            pltpu.VMEM((D, W1), BF16),
+            pltpu.VMEM((D, W2), BF16),
             pltpu.VMEM((ROW, SH, E), BF16),
             pltpu.VMEM((BLK, E), F32),
-            pltpu.VMEM((36, BLK, W1), BF16),
-            pltpu.VMEM((8, BLK, W1), BF16),
-            pltpu.VMEM((BLK, W1), F32),
-            pltpu.VMEM((ROW, SH, W1), F32),
-            pltpu.VMEM((ROW, SH, W1), F32),
+            pltpu.VMEM((36, BLK, W2), BF16),
+            pltpu.VMEM((8, BLK, W2), BF16),
+            pltpu.VMEM((BLK, W2), F32),
+            pltpu.VMEM((ROW, SH, W2), F32),
+            pltpu.VMEM((ROW, SH, W2), F32),
             pltpu.VMEM((R, E), F32),
             pltpu.VMEM((R, E), BF16),
             pltpu.VMEM((R, E), BF16),

time: 85.6 us -> 84.3 us (0.985)
  Pallas kernels: 81.7 us -> 80.3 us
    pallas_call x1, Pallas kernels: 80.6 us -> 79.2 us  [on_device(): pl.pallas_call(kernel, out_shape=(jax.ShapeDtypeStruct((R, D), BF16), jax...]
where the time goes in v6:
time: 84.3 us; the launch traced here: 84.1 us
  Pallas kernels  80.3 us (95%)
  between operations  1.94 us (2%)
  local copies, waits for them, and re-layouts  1.78 us (2%)
    pallas_call x1, Pallas kernels, on_device(): pl.pallas_call(kernel, out_shape=(jax.ShapeDtypeStruct((R, D), BF16), jax...  79.2 us
    unnamed x4, local copies, waits for them, and re-layouts  1.78 us

profile of v6, /device:TPU:1, one launch (start us, length us, event | category | flops | bytes accessed | tf_op | source)
XLA Modules:
  0.0 84.1 jit_solution(5021633994518693808)
XLA Ops:
  1.9 0.0 copy-start
  1.9 1.1 %copy-done = bf16[256,1152]{1,0:T(8,128)(2,1)S(1)} copy-done((bf16[256,1152]{1,0:T(8,128)(2,1)S(1)}, bf16[256,1152]{1,0:T(8,128)(2,1)}, u32[]{:S(2)}) %copy-start) | copy-done | bytes 589848
  3.0 0.0 copy-start.1
  3.0 0.7 copy-done.1
  3.7 79.2 %shard_map.76 = (bf16[256,1536]{1,0:T(8,128)(2,1)S(1)}, bf16[256,1152]{1,0:T(8,128)(2,1)S(1)}, f32[6,1152]{1,0:T(8,128)S(1)}) custom-call(bf16[256,1536]{1,0:T(8,128)(2,1)} %feat_hbm.1, bf16[6,1152]{1,0:T(8,128)(2,1)S(1)} %copy-done.1, bf16[256,1152]{1,0:T(8,128)(2,1)S(1)} %copy-done, f32[1]{0:T(128)S(6)} %copy.8.nef_ref, f32[1]{0:T(128)S(6)} %copy.9.bias_ref), custom_call_target="tpu_custom_call" | custom-call | tf_op jit(solution)/shard_map/pallas_call | solution.py:654
  83.0 1.1 %shard_map.77 = (bf16[256,1536]{1,0:T(8,128)(2,1)}, bf16[256,1152]{1,0:T(8,128)(2,1)}, f32[6,1152]{1,0:T(8,128)}) custom-call(bf16[256,1536]{1,0:T(8,128)(2,1)S(1)} %get-tuple-element.6.gf, bf16[256,1152]{1,0:T(8,128)(2,1)S(1)} %get-tuple-element.7.gt, f32[6,1152]{1,0:T(8,128)S(1)} %get-tuple-element.8.gw), custom_call_target="tpu_custom_call" | custom-call | tf_op jit(solution)/shard_map/pallas_call | solution.py:699
Async XLA Ops:
  1.9 1.1 %copy-start = (bf16[256,1152]{1,0:T(8,128)(2,1)S(1)}, bf16[256,1152]{1,0:T(8,128)(2,1)}, u32[]{:S(2)}) copy-start(bf16[256,1152]{1,0:T(8,128)(2,1)} %text_hbm.1) | copy-start | bytes 1769476
  3.0 0.7 copy-start.1

commit v7 on v6

--- a/solution.py
+++ b/solution.py
@@ -695,7 +695,7 @@
         compiler_params=pltpu.CompilerParams(
             collective_id=0, has_side_effects=True, vmem_limit_bytes=52 * 1024 * 1024
         ),
-    )(image_features, head_weight, text_embeds, natural_exponent_factor, logit_bias)
+    )(*(pltpu.with_memory_space_constraint(a, pltpu.HBM) for a in (image_features, head_weight, text_embeds)), natural_exponent_factor, logit_bias)
     return pl.pallas_call(
         put_out,
         out_shape=tuple(jax.ShapeDtypeStruct(a.shape, a.dtype) for a in results),

time: 84.3 us -> 82.4 us (0.977)
  local copies, waits for them, and re-layouts: 1.78 us -> 0 us
    unnamed x4 -> x0, local copies, waits for them, and re-layouts: 1.78 us -> none
where the time goes in v7:
time: 82.4 us; the launch traced here: 82.3 us
  Pallas kernels  80.4 us (98%)
  between operations  1.93 us (2%)
    pallas_call x1, Pallas kernels, on_device(): pl.pallas_call(kernel, out_shape=(jax.ShapeDtypeStruct((R, D), BF16), jax...  79.3 us

profile of v7, /device:TPU:1, one launch (start us, length us, event | category | flops | bytes accessed | tf_op | source)
XLA Modules:
  0.0 82.3 jit_solution(7466289752907650071)
XLA Ops:
  1.9 79.3 %shard_map.76 = (bf16[256,1536]{1,0:T(8,128)(2,1)S(1)}, bf16[256,1152]{1,0:T(8,128)(2,1)S(1)}, f32[6,1152]{1,0:T(8,128)S(1)}) custom-call(bf16[256,1536]{1,0:T(8,128)(2,1)} %feat_hbm.1, bf16[6,1152]{1,0:T(8,128)(2,1)} %w_hbm.1, bf16[256,1152]{1,0:T(8,128)(2,1)} %text_hbm.1, f32[1]{0:T(128)S(6)} %copy.8.nef_ref, f32[1]{0:T(128)S(6)} %copy.9.bias_ref), custom_call_target="tpu_custom_call" | custom-call | tf_op jit(solution)/shard_map/pallas_call | solution.py:654
  81.2 1.1 %shard_map.77 = (bf16[256,1536]{1,0:T(8,128)(2,1)}, bf16[256,1152]{1,0:T(8,128)(2,1)}, f32[6,1152]{1,0:T(8,128)}) custom-call(bf16[256,1536]{1,0:T(8,128)(2,1)S(1)} %get-tuple-element.6.gf, bf16[256,1152]{1,0:T(8,128)(2,1)S(1)} %get-tuple-element.7.gt, f32[6,1152]{1,0:T(8,128)S(1)} %get-tuple-element.8.gw), custom_call_target="tpu_custom_call" | custom-call | tf_op jit(solution)/shard_map/pallas_call | solution.py:699

commit v8 on v7

--- a/solution.py
+++ b/solution.py
@@ -509,10 +509,9 @@
             for k in Z_ARRIVAL[1:]:
                 total = total + take(24 + k)
         else:
-            for j in range(NY):
-                product(j)
             order = (2, 1, 3, 0)
             for j in order:
+                product(j)
                 emit(mine(j, 4), 16 + j, 0, -1)
             feature_gradient(2)
             for h in (3, 2, 1):

time: 82.4 us -> 82.3 us (level)
  no operation moved by 1% of the time
where the time goes in v8:
time: 82.3 us; the launch traced here: 82.2 us
  Pallas kernels  80.3 us (98%)
  between operations  1.93 us (2%)
    pallas_call x1, Pallas kernels, on_device(): pl.pallas_call(kernel, out_shape=(jax.ShapeDtypeStruct((R, D), BF16), jax...  79.2 us

profile of v8, /device:TPU:1, one launch (start us, length us, event | category | flops | bytes accessed | tf_op | source)
XLA Modules:
  0.0 82.2 jit_solution(14956471982167443077)
XLA Ops:
  1.9 79.2 %shard_map.76 = (bf16[256,1536]{1,0:T(8,128)(2,1)S(1)}, bf16[256,1152]{1,0:T(8,128)(2,1)S(1)}, f32[6,1152]{1,0:T(8,128)S(1)}) custom-call(bf16[256,1536]{1,0:T(8,128)(2,1)} %feat_hbm.1, bf16[6,1152]{1,0:T(8,128)(2,1)} %w_hbm.1, bf16[256,1152]{1,0:T(8,128)(2,1)} %text_hbm.1, f32[1]{0:T(128)S(6)} %copy.8.nef_ref, f32[1]{0:T(128)S(6)} %copy.9.bias_ref), custom_call_target="tpu_custom_call" | custom-call | tf_op jit(solution)/shard_map/pallas_call | solution.py:653
  81.1 1.1 %shard_map.77 = (bf16[256,1536]{1,0:T(8,128)(2,1)}, bf16[256,1152]{1,0:T(8,128)(2,1)}, f32[6,1152]{1,0:T(8,128)}) custom-call(bf16[256,1536]{1,0:T(8,128)(2,1)S(1)} %get-tuple-element.6.gf, bf16[256,1152]{1,0:T(8,128)(2,1)S(1)} %get-tuple-element.7.gt, f32[6,1152]{1,0:T(8,128)S(1)} %get-tuple-element.8.gw), custom_call_target="tpu_custom_call" | custom-call | tf_op jit(solution)/shard_map/pallas_call | solution.py:698
